TPU v7x, 8 devices: a whole 2x2x1 slice. The times are simulated.
8 devices in a mesh: tp: 2 (over z, y), cp: 4 (over x, core).
Axes of the slice: x: 2, y: 2, z: 1, core: 2. Of those that a mesh axis runs over, the one named last changes fastest.
Arguments:
- hidden: bfloat16 [16, 2048, 2048], P(None, 'cp')
- grad_out: bfloat16 [16, 2048, 2048], P(None, 'cp')
- w_query: bfloat16 [2048, 8, 256], P(None, 'tp')
- w_key: bfloat16 [2048, 256], replicated
- w_value: bfloat16 [2048, 256], replicated
- w_out: bfloat16 [8, 256, 2048], P('tp')
Outputs:
- output 1: bfloat16 [16, 2048, 2048], P(None, 'cp')
- output 2: bfloat16 [16, 2048, 2048], P(None, 'cp')
- output 3: float32 [2048, 8, 256], P(None, 'tp')
- output 4: float32 [2048, 256], replicated
- output 5: float32 [2048, 256], replicated
- output 6: float32 [8, 256, 2048], P('tp')
All inputs are finite; a program needn't handle non-finite values.
Results may differ from a plain program's by a relative error of at most 0.0110002.
Values are sent between devices in bfloat16 or wider.
A program may use at most 1 GiB of HBM per device.

v0:
```python
import jax
import jax.numpy as jnp
from jax import lax
from jax.sharding import PartitionSpec as P

ROPE_BASE = 10000.0


def rope_tables(positions, head_dim):
    half_dim = head_dim // 2
    inv_freq = 1.0 / jnp.power(ROPE_BASE, jnp.arange(half_dim, dtype=jnp.float32) * (2.0 / head_dim))
    angles = positions.astype(jnp.float32)[:, None] * inv_freq[None, :]
    return jnp.cos(angles), jnp.sin(angles)


def rotate(rot_in, cos_tab, sin_tab):
    half_dim = rot_in.shape[-1] // 2
    low_half = rot_in[..., :half_dim]
    high_half = rot_in[..., half_dim:]
    return jnp.concatenate([low_half * cos_tab - high_half * sin_tab, high_half * cos_tab + low_half * sin_tab], axis=-1)


def unrotate(rot_in, cos_tab, sin_tab):
    half_dim = rot_in.shape[-1] // 2
    low_half = rot_in[..., :half_dim]
    high_half = rot_in[..., half_dim:]
    return jnp.concatenate([low_half * cos_tab + high_half * sin_tab, high_half * cos_tab - low_half * sin_tab], axis=-1)


def pair_scores(queries, key_blk, q_start, k_start):
    scores = jnp.einsum("bhqe,bke->bhqk", queries, key_blk, preferred_element_type=jnp.float32)
    q_pos = q_start + jnp.arange(queries.shape[2])
    k_pos = k_start + jnp.arange(key_blk.shape[1])
    allowed = k_pos[None, :] <= q_pos[:, None]
    return jnp.where(allowed, scores, -jnp.inf)


def forward_update(queries, kv_blk, q_start, k_start, soft_stats):
    run_max, run_sum, run_acc = soft_stats
    scores = pair_scores(queries, kv_blk[:, 0], q_start, k_start)
    new_max = jnp.maximum(run_max, jnp.max(scores, axis=-1))
    rescale = jnp.exp(run_max - new_max)
    weights = jnp.exp(scores - new_max[..., None])
    new_sum = run_sum * rescale + jnp.sum(weights, axis=-1)
    new_acc = run_acc * rescale[..., None] + jnp.einsum("bhqk,bke->bhqe", weights.astype(jnp.bfloat16), kv_blk[:, 1], preferred_element_type=jnp.float32)
    return new_max, new_sum, new_acc


def backward_update(queries, d_out, row_lse, row_delta, kv_blk, q_start, k_start):
    scores = pair_scores(queries, kv_blk[:, 0], q_start, k_start)
    prob_blk = jnp.exp(scores - row_lse[..., None])
    d_prob = jnp.einsum("bhqe,bke->bhqk", d_out, kv_blk[:, 1], preferred_element_type=jnp.float32)
    d_score = (prob_blk * (d_prob - row_delta[..., None])).astype(jnp.bfloat16)
    dq_part = jnp.einsum("bhqk,bke->bhqe", d_score, kv_blk[:, 0], preferred_element_type=jnp.float32)
    dk_part = jnp.einsum("bhqk,bhqe->bke", d_score, queries, preferred_element_type=jnp.float32)
    dv_part = jnp.einsum("bhqk,bhqe->bke", prob_blk.astype(jnp.bfloat16), d_out, preferred_element_type=jnp.float32)
    return dq_part, jnp.stack([dk_part, dv_part], axis=1)


def solution(mesh):
    cp_size = mesh.shape["cp"]
    shift_pairs = [(src_idx, (src_idx + 1) % cp_size) for src_idx in range(cp_size)]

    def local_program(hidden, grad_out, w_query, w_key, w_value, w_out):
        n_batch, block_len = hidden.shape[0], hidden.shape[1]
        n_local = w_query.shape[1]
        head_dim = w_key.shape[1]
        q_scale = head_dim ** -0.5
        cp_idx = lax.axis_index("cp")
        q_start = cp_idx * block_len
        cos_tab, sin_tab = rope_tables(q_start + jnp.arange(block_len), head_dim)
        q_pre = jnp.einsum("bsd,dhe->bhse", hidden, w_query, preferred_element_type=jnp.float32)
        queries = (rotate(q_pre, cos_tab, sin_tab) * q_scale).astype(jnp.bfloat16)
        key_pre = jnp.einsum("bsd,de->bse", hidden, w_key, preferred_element_type=jnp.float32)
        key_loc = rotate(key_pre, cos_tab, sin_tab).astype(jnp.bfloat16)
        val_loc = jnp.einsum("bsd,de->bse", hidden, w_value, preferred_element_type=jnp.float32).astype(jnp.bfloat16)
        kv_loc = jnp.stack([key_loc, val_loc], axis=1)

        def fwd_compute(step_idx, kv_blk, soft_stats):
            k_start = ((cp_idx - step_idx) % cp_size) * block_len
            return lax.cond(step_idx <= cp_idx, lambda stats_in: forward_update(queries, kv_blk, q_start, k_start, stats_in), lambda stats_in: stats_in, soft_stats)

        def fwd_body(step_idx, loop_state):
            kv_blk, soft_stats = loop_state
            soft_stats = fwd_compute(step_idx, kv_blk, soft_stats)
            return lax.ppermute(kv_blk, "cp", shift_pairs), soft_stats

        stats_init = (jnp.full((n_batch, n_local, block_len), -jnp.inf, jnp.float32), jnp.zeros((n_batch, n_local, block_len), jnp.float32), jnp.zeros((n_batch, n_local, block_len, head_dim), jnp.float32))
        kv_blk, soft_stats = lax.fori_loop(0, cp_size - 1, fwd_body, (kv_loc, stats_init))
        run_max, run_sum, run_acc = fwd_compute(cp_size - 1, kv_blk, soft_stats)
        attn_heads = (run_acc / run_sum[..., None]).astype(jnp.bfloat16)
        row_lse = run_max + jnp.log(run_sum)
        out_part = jnp.einsum("cirf,ife->cre", attn_heads, w_out, preferred_element_type=jnp.float32)
        attn_out = lax.psum(out_part, "tp").astype(jnp.bfloat16)
        d_out = jnp.einsum("cre,ife->cirf", grad_out, w_out, preferred_element_type=jnp.float32).astype(jnp.bfloat16)
        row_delta = jnp.einsum("bhqe,bhqe->bhq", d_out, attn_heads, preferred_element_type=jnp.float32)

        def bwd_compute(step_idx, kv_blk, dkv_blk, dq_acc):
            k_start = ((cp_idx - step_idx) % cp_size) * block_len

            def active(acc_pair):
                dq_in, dkv_in = acc_pair
                dq_part, dkv_part = backward_update(queries, d_out, row_lse, row_delta, kv_blk, q_start, k_start)
                return dq_in + dq_part, dkv_in + dkv_part

            return lax.cond(step_idx <= cp_idx, active, lambda acc_pair: acc_pair, (dq_acc, dkv_blk))

        def bwd_body(step_idx, loop_state):
            kv_blk, dkv_blk, dq_acc = loop_state
            dq_acc, dkv_blk = bwd_compute(step_idx, kv_blk, dkv_blk, dq_acc)
            kv_blk = lax.ppermute(kv_blk, "cp", shift_pairs)
            dkv_blk = lax.ppermute(dkv_blk, "cp", shift_pairs)
            return kv_blk, dkv_blk, dq_acc

        dkv_init = jnp.zeros((n_batch, 2, block_len, head_dim), jnp.float32)
        dq_init = jnp.zeros((n_batch, n_local, block_len, head_dim), jnp.float32)
        kv_blk, dkv_blk, dq_acc = lax.fori_loop(0, cp_size - 1, bwd_body, (kv_loc, dkv_init, dq_init))
        dq_acc, dkv_blk = bwd_compute(cp_size - 1, kv_blk, dkv_blk, dq_acc)
        dkv_blk = lax.ppermute(dkv_blk, "cp", shift_pairs)
        dkv_full = lax.psum(dkv_blk, "tp")
        dq_pre = (unrotate(dq_acc, cos_tab, sin_tab) * q_scale).astype(jnp.bfloat16)
        dk_pre = unrotate(dkv_full[:, 0], cos_tab, sin_tab).astype(jnp.bfloat16)
        dv_pre = dkv_full[:, 1].astype(jnp.bfloat16)
        d_w_query = lax.psum(jnp.einsum("cre,cirf->eif", hidden, dq_pre, preferred_element_type=jnp.float32), "cp")
        d_w_out = lax.psum(jnp.einsum("cirf,cre->ife", attn_heads, grad_out, preferred_element_type=jnp.float32), "cp")
        d_w_key = lax.psum(jnp.einsum("cre,crf->ef", hidden, dk_pre, preferred_element_type=jnp.float32), "cp")
        d_w_value = lax.psum(jnp.einsum("cre,crf->ef", hidden, dv_pre, preferred_element_type=jnp.float32), "cp")
        dh_heads = lax.psum(jnp.einsum("cirf,eif->cre", dq_pre, w_query, preferred_element_type=jnp.float32), "tp")
        dh_kv = jnp.einsum("crf,ef->cre", dk_pre, w_key, preferred_element_type=jnp.float32) + jnp.einsum("crf,ef->cre", dv_pre, w_value, preferred_element_type=jnp.float32)
        d_hidden = (dh_heads + dh_kv).astype(jnp.bfloat16)
        return attn_out, d_hidden, d_w_query, d_w_key, d_w_value, d_w_out

    row_spec = P(None, "cp", None)
    return jax.shard_map(local_program, mesh=mesh, in_specs=(row_spec, row_spec, P(None, "tp", None), P(), P(), P("tp", None, None)), out_specs=(row_spec, row_spec, P(None, "tp", None), P(), P(), P("tp", None, None)), check_vma=False)
```

profile of v0, /device:TPU:0, one launch (start us, length us, event | category | flops | bytes accessed | tf_op | source)
XLA Modules:
  0.0 5962.8 jit_solution(16542599882374469416)
XLA Ops:
  7.3 42.2 convert_bitcast_fusion
  49.5 24.8 copy.71
  74.3 23.6 copy.26
  98.9 42.2 fusion.85
  141.1 17.3 multiply_subtract_fusion.1
  158.4 15.4 fusion.75
  173.8 23.6 copy.22
  197.4 14.3 fusion.109
  213.2 15.1 convert_bitcast_fusion.1
  232.0 11.8 copy.21
  251.3 11.3 broadcast.147.clone
  262.7 310.9 %while.40 = (s32[]{:T(128)}, bf16[16,2,512,256]{3,2,0,1:T(8,128)(2,1)}, f32[16,4,512]{2,1,0:T(4,128)S(1)}, f32[16,4,512]{2,1,0:T(4,128)S(1)}, f32[16,4,512,256]{...) while((s32[]{:T(128)}, bf16[16,2,512,256]{3,2,0,1:T(8,128)(2,1)}, ...), condition=%wide.region_5.6_spmd, body=%wide.region_0.5_spmd.sunk | while | flops 17331191808 | bytes 347087232 | solution.py:89
  262.7 7.7 copy.125
  271.2 97.0 %conditional.8 = ((f32[16,4,512]{2,1,0:T(4,128)S(1)}, f32[16,4,512]{2,1,0:T(4,128)S(1)}, f32[16,4,512,256]{3,2,1,0:T(8,128)})) conditional(s32[]{:T(128)} %convert_element_type.152, (f32[16,4,512]{2,1,0:T(4,128)S(1)}, f32[16,4,512]{2,1,0:T(4,128)S(1)}, f32[16,4,512,256]{3,2,1,0:T(8,128)}) %tuple.205, (s32[]{:T(128)}, s32[]{:T(128)}, s32[]{:T(128)}, ...), branch_computations={%region_1.1_spmd, %region_2.4_spmd} | conditional | flops 17331191808 | bytes 296755360 | solution.py:81
  271.4 30.3 select_reduce_fusion
  301.8 21.5 fusion.1
  323.4 44.8 multiply_add_fusion
  368.2 7.7 copy.125
  378.5 90.5 %collective-permute-done = bf16[16,2,512,256]{3,2,0,1:T(8,128)(2,1)} collective-permute-done((bf16[16,2,512,256]{3,2,0,1:T(8,128)(2,1)}, bf16[16,2,512,256]{3,2,0,1:T(8,128)(2,1)}, u32[]{:S(2)}, u32[]{:S(2)}) %collective-permute-start) | collective-permute-done | bytes 8388640 | tf_op jit(solution)/shard_map/while/body/eval_jaxpr/ppermute | solution.py:86
  483.2 90.5 %collective-permute-done = bf16[16,2,512,256]{3,2,0,1:T(8,128)(2,1)} collective-permute-done((bf16[16,2,512,256]{3,2,0,1:T(8,128)(2,1)}, bf16[16,2,512,256]{3,2,0,1:T(8,128)(2,1)}, u32[]{:S(2)}, u32[]{:S(2)}) %collective-permute-start) | collective-permute-done | bytes 8388640 | tf_op jit(solution)/shard_map/while/body/eval_jaxpr/ppermute | solution.py:86
  573.6 27.5 multiply_reduce_fusion
  601.2 11.3 broadcast.147
  612.5 7.7 broadcast_in_dim.86
  620.2 1482.6 %while.41 = (s32[]{:T(128)}, bf16[16,2,512,256]{3,2,0,1:T(8,128)(2,1)}, f32[16,2,512,256]{3,2,0,1:T(8,128)}, f32[16,4,512,256]{3,2,1,0:T(8,128)}, s32[]{:T(128)}...) while((s32[]{:T(128)}, ...), condition=%wide.region_14.15_spmd, body=%wide.region_11.14_spmd.sunk | while | flops 43100930048 | bytes 668082624 | solution.py:117
  620.4 7.7 copy.146
  628.0 181.9 %conditional.9 = ((f32[16,4,512,256]{3,2,1,0:T(8,128)}, f32[16,2,512,256]{3,2,0,1:T(8,128)})) conditional(s32[]{:T(128)} %convert_element_type.153, (f32[16,4,512,256]{3,2,1,0:T(8,128)}, f32[16,2,512,256]{3,2,0,1:T(8,128)}) %tuple.208, (s32[]{:T(128)}, s32[]{:T(128)}, s32[]{:T(128)}, bf16[16,2,512,256]{3,2,0,1:T(8,128)(2,1)}, ...), branch_computations={%region_12.12_spmd, %region_13.13_spmd} | conditional | flops 43100930048 | bytes 517087424 | solution.py:106
  628.2 30.1 fusion.23
  658.3 40.9 multiply_convert_fusion
  699.2 23.0 convolution_bitcast_fusion
  722.3 33.6 fusion.28
  755.8 17.9 maximum_add_fusion
  773.7 36.2 convolution_add_fusion
  816.5 276.7 %collective-permute-done.2 = f32[16,2,512,256]{3,2,0,1:T(8,128)} collective-permute-done((f32[16,2,512,256]{3,2,0,1:T(8,128)}, f32[16,2,512,256]{3,2,0,1:T(8,128)}, u32[]{:S(2)}, u32[]{:S(2)}) %collective-permute-start.2) | collective-permute-done | bytes 16777248 | tf_op jit(solution)/shard_map/while/body/eval_jaxpr/ppermute | solution.py:112
  1093.2 11.3 copy.151
  1104.5 78.6 %collective-permute-done.1 = bf16[16,2,512,256]{3,2,0,1:T(8,128)(2,1)} collective-permute-done((bf16[16,2,512,256]{3,2,0,1:T(8,128)(2,1)}, bf16[16,2,512,256]{3,2,0,1:T(8,128)(2,1)}, u32[]{:S(2)}, u32[]{:S(2)}) %collective-permute-start.1) | collective-permute-done | bytes 8388640 | tf_op jit(solution)/shard_map/while/body/eval_jaxpr/ppermute | solution.py:111
  1183.1 7.7 copy.146
  1190.7 85.4 %collective-permute-start.2 = (f32[16,2,512,256]{3,2,0,1:T(8,128)}, f32[16,2,512,256]{3,2,0,1:T(8,128)}, u32[]{:S(2)}, u32[]{:S(2)}) collective-permute-start(f32[16,2,512,256]{3,2,0,1:T(8,128)} %get-tuple-element.1103), channel_id=1, source_target_pairs={{0,1},{1,2},{2,3},{3,0},{4,5},{5,6},{6,7},{7,4}} | collective-permute-start | bytes 50331656 | tf_op jit(solution)/shard_map/while/body/eval_jaxpr/ppermute | solution.py:112
  1278.6 274.2 %collective-permute-done.2 = f32[16,2,512,256]{3,2,0,1:T(8,128)} collective-permute-done((f32[16,2,512,256]{3,2,0,1:T(8,128)}, f32[16,2,512,256]{3,2,0,1:T(8,128)}, u32[]{:S(2)}, u32[]{:S(2)}) %collective-permute-start.2) | collective-permute-done | bytes 16777248 | tf_op jit(solution)/shard_map/while/body/eval_jaxpr/ppermute | solution.py:112
  1552.8 11.3 copy.151
  1564.2 78.6 %collective-permute-done.1 = bf16[16,2,512,256]{3,2,0,1:T(8,128)(2,1)} collective-permute-done((bf16[16,2,512,256]{3,2,0,1:T(8,128)(2,1)}, bf16[16,2,512,256]{3,2,0,1:T(8,128)(2,1)}, u32[]{:S(2)}, u32[]{:S(2)}) %collective-permute-start.1) | collective-permute-done | bytes 8388640 | tf_op jit(solution)/shard_map/while/body/eval_jaxpr/ppermute | solution.py:111
  1650.4 90.4 %collective-permute-start.1 = (bf16[16,2,512,256]{3,2,0,1:T(8,128)(2,1)}, bf16[16,2,512,256]{3,2,0,1:T(8,128)(2,1)}, u32[]{:S(2)}, u32[]{:S(2)}) collective-permute-start(bf16[16,2,512,256]{3,2,0,1:T(8,128)(2,1)} %copy.146), channel_id=1, source_target_pairs={{0,1},{1,2},{2,3},{3,0},{4,5},{5,6},{6,7},{7,4}} | collective-permute-start | bytes 25165832 | tf_op jit(solution)/shard_map/while/body/eval_jaxpr/ppermute | solution.py:111
  1740.8 271.7 %collective-permute-done.2 = f32[16,2,512,256]{3,2,0,1:T(8,128)} collective-permute-done((f32[16,2,512,256]{3,2,0,1:T(8,128)}, f32[16,2,512,256]{3,2,0,1:T(8,128)}, u32[]{:S(2)}, u32[]{:S(2)}) %collective-permute-start.2) | collective-permute-done | bytes 16777248 | tf_op jit(solution)/shard_map/while/body/eval_jaxpr/ppermute | solution.py:112
  2012.5 11.3 copy.151
  2023.8 78.6 %collective-permute-done.1 = bf16[16,2,512,256]{3,2,0,1:T(8,128)(2,1)} collective-permute-done((bf16[16,2,512,256]{3,2,0,1:T(8,128)(2,1)}, bf16[16,2,512,256]{3,2,0,1:T(8,128)(2,1)}, u32[]{:S(2)}, u32[]{:S(2)}) %collective-permute-start.1) | collective-permute-done | bytes 8388640 | tf_op jit(solution)/shard_map/while/body/eval_jaxpr/ppermute | solution.py:111
  2108.5 18.0 copy.35
  2126.5 21.5 fusion.119
  2148.1 16.4 copy.29
  2164.5 16.4 copy.30
  2180.9 23.0 multiply_add_fusion.4
  2203.9 44.8 convolution_bitcast_fusion.1
  2248.7 235.2 %collective-permute-done.3 = f32[16,2,512,256]{2,3,0,1:T(8,128)} collective-permute-done((f32[16,2,512,256]{2,3,0,1:T(8,128)}, f32[16,2,512,256]{2,3,0,1:T(8,128)}, u32[]{:S(2)}, u32[]{:S(2)}) %collective-permute-start.3) | collective-permute-done | bytes 16777248 | tf_op jit(solution)/shard_map/ppermute | solution.py:119
  2484.2 44.9 convolution_bitcast_fusion.2
  2529.1 19.3 fusion.156
  2550.7 40.4 fusion.93
  2591.0 43.9 fusion.90
  2635.0 1660.4 %all-reduce.8.cloned.1.call-done = (f32[16,512,2048]{2,1,0:T(8,128)}, f32[16,2,512,256]{2,3,0,1:T(8,128)}) async-done(((f32[16,512,2048]{2,1,0:T(8,128)}, f32[16,2,512,256]{2,3,0,1:T(8,128)}), (f32[16,512,2048]{2,1,0:T(8,128)}, f32[16,2,512,256]{2,3,0,1:T(8,128)})) %all-reduce.8.cloned.1.call-update) | async-done | bytes 83886096 | tf_op jit(solution)/shard_map/psum | solution.py:128
  4295.4 8.1 slice_bitcast_fusion
  4303.5 18.4 convolution_bitcast_fusion.3
  4328.2 15.7 convolution_bitcast_fusion.4
  4343.9 1508.3 %all-reduce.9 = bf16[16,512,2048]{2,1,0:T(8,128)(2,1)} all-reduce(f32[16,512,2048]{2,1,0:T(8,128)} %convolution_bitcast_fusion.2), channel_id=1, replica_groups=mesh['tp'=2,'cp'=4] {'tp'}, use_global_device_ids=true, to_apply=%region_10.11 | all-reduce | flops 16777216 | bytes 100663296 | tf_op jit(solution)/shard_map/psum | solution.py:94
  5852.2 24.7 fusion.101
  5876.9 56.2 add_convert_fusion
  5933.2 10.0 copy.39
  5947.9 7.9 copy.166
  (63 shorter events, 68.0 us)
Async XLA Ops:
  7.2 190.2 %copy-start = (bf16[2048,256]{1,0:T(8,128)(2,1)S(1)}, bf16[2048,256]{1,0:T(8,128)(2,1)}, u32[]{:S(2)}) copy-start(bf16[2048,256]{1,0:T(8,128)(2,1)} %param.21) | copy-start | bytes 3145732
  7.2 4288.2 %all-reduce.8.cloned.1.call-start = ((), (), s32[]{:S(2)}) async-start(), calls=%async_computation.1 | async-start | bytes 167772160 | tf_op jit(solution)/shard_map/psum | solution.py:128
  98.8 112.8 %copy-start.4 = (f32[512,128]{0,1:T(8,128)}, f32[512,128]{0,1:T(8,128)S(1)}, u32[]{:S(2)}) copy-start(f32[512,128]{0,1:T(8,128)S(1)} %get-tuple-element.979) | copy-start | bytes 786436
  98.9 112.8 %copy-start.7 = (f32[512,128]{0,1:T(8,128)}, f32[512,128]{0,1:T(8,128)S(1)}, u32[]{:S(2)}) copy-start(f32[512,128]{0,1:T(8,128)S(1)} %get-tuple-element.980) | copy-start | bytes 786436
  197.4 15.8 copy-start.10
  270.4 97.9 %collective-permute-start = (bf16[16,2,512,256]{3,2,0,1:T(8,128)(2,1)}, bf16[16,2,512,256]{3,2,0,1:T(8,128)(2,1)}, u32[]{:S(2)}, u32[]{:S(2)}) collective-permute-start(bf16[16,2,512,256]{3,2,0,1:T(8,128)(2,1)} %copy.125), channel_id=1, source_target_pairs={{0,1},{1,2},{2,3},{3,0},{4,5},{5,6},{6,7},{7,4}} | collective-permute-start | bytes 25165832 | tf_op jit(solution)/shard_map/while/body/eval_jaxpr/ppermute | solution.py:86
  375.9 93.1 %collective-permute-start = (bf16[16,2,512,256]{3,2,0,1:T(8,128)(2,1)}, bf16[16,2,512,256]{3,2,0,1:T(8,128)(2,1)}, u32[]{:S(2)}, u32[]{:S(2)}) collective-permute-start(bf16[16,2,512,256]{3,2,0,1:T(8,128)(2,1)} %copy.125), channel_id=1, source_target_pairs={{0,1},{1,2},{2,3},{3,0},{4,5},{5,6},{6,7},{7,4}} | collective-permute-start | bytes 25165832 | tf_op jit(solution)/shard_map/while/body/eval_jaxpr/ppermute | solution.py:86
  476.6 97.0 %collective-permute-start = (bf16[16,2,512,256]{3,2,0,1:T(8,128)(2,1)}, bf16[16,2,512,256]{3,2,0,1:T(8,128)(2,1)}, u32[]{:S(2)}, u32[]{:S(2)}) collective-permute-start(bf16[16,2,512,256]{3,2,0,1:T(8,128)(2,1)} %copy.125), channel_id=1, source_target_pairs={{0,1},{1,2},{2,3},{3,0},{4,5},{5,6},{6,7},{7,4}} | collective-permute-start | bytes 25165832 | tf_op jit(solution)/shard_map/while/body/eval_jaxpr/ppermute | solution.py:86
  809.9 283.3 %collective-permute-start.2 = (f32[16,2,512,256]{3,2,0,1:T(8,128)}, f32[16,2,512,256]{3,2,0,1:T(8,128)}, u32[]{:S(2)}, u32[]{:S(2)}) collective-permute-start(f32[16,2,512,256]{3,2,0,1:T(8,128)} %get-tuple-element.1103), channel_id=1, source_target_pairs={{0,1},{1,2},{2,3},{3,0},{4,5},{5,6},{6,7},{7,4}} | collective-permute-start | bytes 50331656 | tf_op jit(solution)/shard_map/while/body/eval_jaxpr/ppermute | solution.py:112
  809.9 373.2 %collective-permute-start.1 = (bf16[16,2,512,256]{3,2,0,1:T(8,128)(2,1)}, bf16[16,2,512,256]{3,2,0,1:T(8,128)(2,1)}, u32[]{:S(2)}, u32[]{:S(2)}) collective-permute-start(bf16[16,2,512,256]{3,2,0,1:T(8,128)(2,1)} %copy.146), channel_id=1, source_target_pairs={{0,1},{1,2},{2,3},{3,0},{4,5},{5,6},{6,7},{7,4}} | collective-permute-start | bytes 25165832 | tf_op jit(solution)/shard_map/while/body/eval_jaxpr/ppermute | solution.py:111
  1190.7 362.1 %collective-permute-start.2 = (f32[16,2,512,256]{3,2,0,1:T(8,128)}, f32[16,2,512,256]{3,2,0,1:T(8,128)}, u32[]{:S(2)}, u32[]{:S(2)}) collective-permute-start(f32[16,2,512,256]{3,2,0,1:T(8,128)} %get-tuple-element.1103), channel_id=1, source_target_pairs={{0,1},{1,2},{2,3},{3,0},{4,5},{5,6},{6,7},{7,4}} | collective-permute-start | bytes 50331656 | tf_op jit(solution)/shard_map/while/body/eval_jaxpr/ppermute | solution.py:112
  1276.1 366.6 %collective-permute-start.1 = (bf16[16,2,512,256]{3,2,0,1:T(8,128)(2,1)}, bf16[16,2,512,256]{3,2,0,1:T(8,128)(2,1)}, u32[]{:S(2)}, u32[]{:S(2)}) collective-permute-start(bf16[16,2,512,256]{3,2,0,1:T(8,128)(2,1)} %copy.146), channel_id=1, source_target_pairs={{0,1},{1,2},{2,3},{3,0},{4,5},{5,6},{6,7},{7,4}} | collective-permute-start | bytes 25165832 | tf_op jit(solution)/shard_map/while/body/eval_jaxpr/ppermute | solution.py:111
  1650.4 362.1 %collective-permute-start.2 = (f32[16,2,512,256]{3,2,0,1:T(8,128)}, f32[16,2,512,256]{3,2,0,1:T(8,128)}, u32[]{:S(2)}, u32[]{:S(2)}) collective-permute-start(f32[16,2,512,256]{3,2,0,1:T(8,128)} %get-tuple-element.1103), channel_id=1, source_target_pairs={{0,1},{1,2},{2,3},{3,0},{4,5},{5,6},{6,7},{7,4}} | collective-permute-start | bytes 50331656 | tf_op jit(solution)/shard_map/while/body/eval_jaxpr/ppermute | solution.py:112
  1650.4 452.0 %collective-permute-start.1 = (bf16[16,2,512,256]{3,2,0,1:T(8,128)(2,1)}, bf16[16,2,512,256]{3,2,0,1:T(8,128)(2,1)}, u32[]{:S(2)}, u32[]{:S(2)}) collective-permute-start(bf16[16,2,512,256]{3,2,0,1:T(8,128)(2,1)} %copy.146), channel_id=1, source_target_pairs={{0,1},{1,2},{2,3},{3,0},{4,5},{5,6},{6,7},{7,4}} | collective-permute-start | bytes 25165832 | tf_op jit(solution)/shard_map/while/body/eval_jaxpr/ppermute | solution.py:111
  2126.5 357.4 %collective-permute-start.3 = (f32[16,2,512,256]{2,3,0,1:T(8,128)}, f32[16,2,512,256]{2,3,0,1:T(8,128)}, u32[]{:S(2)}, u32[]{:S(2)}) collective-permute-start(f32[16,2,512,256]{2,3,0,1:T(8,128)} %copy.35), channel_id=1, source_target_pairs={{0,1},{1,2},{2,3},{3,0},{4,5},{5,6},{6,7},{7,4}} | collective-permute-start | bytes 50331656 | tf_op jit(solution)/shard_map/ppermute | solution.py:119
  2164.5 16.4 copy-start.5
  2164.5 16.4 copy-start.8
  2180.9 23.0 copy-start.11
  2483.9 3449.2 %all-reduce.6.cloned.1.call-start = ((), (), s32[]{:S(2)}) async-start(), calls=%async_computation | async-start | bytes 41943040 | tf_op jit(solution)/shard_map/psum | solution.py:124
  2529.1 21.6 copy-start.1
  4303.5 18.5 copy-start.6
  4326.9 1.3 copy-start.2
  5933.1 12.9 copy-start.9
Sparse Core Ops, SparseCore 0:
  2484.0 1811.3 all-reduce.7
  4344.1 352.6 all-reduce.5
where the time goes:
time: 5980 us; the launch traced here: 5960 us
  waiting for transfers between devices  3130 us (52%)
  blocking collectives  1510 us (25%)
  matrix products  642 us (11%)
  local copies, waits for them, and re-layouts  308 us (5%)
  starting transfers between devices  195 us (3%)
  other arithmetic  154 us (3%)
    psum x1, waiting for transfers between devices, local_program(): lax.psum(jnp.einsum('cirf,eif->cre', dq_pre, w_query, preferred_element_t...  1660 us
    psum x1, blocking collectives, local_program(): attn_out = lax.psum(out_part, 'tp').astype(jnp.bfloat16)  1510 us
    ppermute x3, waiting for transfers between devices, bwd_body(): dkv_blk = lax.ppermute(dkv_blk, 'cp', shift_pairs)  823 us
    ppermute x3, waiting for transfers between devices, bwd_body(): kv_blk = lax.ppermute(kv_blk, 'cp', shift_pairs)  236 us
    ppermute x1, waiting for transfers between devices, local_program(): dkv_blk = lax.ppermute(dkv_blk, 'cp', shift_pairs)  235 us
    ppermute x3, waiting for transfers between devices, fwd_body(): return (lax.ppermute(kv_blk, 'cp', shift_pairs), soft_stats)  181 us
  transfers between devices with their start and end apart: 12, of which 10 were waited for; matrix products, arithmetic and copies ran while one was open for 8% of the time, Pallas kernels for 0%

commit v1 on v0

v1 whole, which is shorter than its diff:
```python
import functools

import jax
import jax.numpy as jnp
from jax import lax
from jax.experimental import pallas as pl
from jax.experimental.pallas import tpu as pltpu
from jax.sharding import PartitionSpec as P


ROPE_BASE = 10000.0
F32 = jnp.float32
BF16 = jnp.bfloat16
HPS = 2
HPF = 4
E = 256
S = 512
HALF = 256


def rope_tables(positions, head_dim):
    half_dim = head_dim // 2
    inv_freq = 1.0 / jnp.power(ROPE_BASE, jnp.arange(half_dim, dtype=F32) * (2.0 / head_dim))
    angles = positions.astype(F32)[:, None] * inv_freq[None, :]
    return jnp.cos(angles), jnp.sin(angles)


def rot(x, cos, sin):
    h = x.shape[-1] // 2
    a, b = x[..., :h], x[..., h:]
    return jnp.concatenate([a * cos - b * sin, b * cos + a * sin], axis=-1)


def unrot(x, cos, sin):
    h = x.shape[-1] // 2
    a, b = x[..., :h], x[..., h:]
    return jnp.concatenate([a * cos + b * sin, b * cos - a * sin], axis=-1)


def dot_nt(a, b):
    return lax.dot_general(a, b, (((1,), (1,)), ((), ())), preferred_element_type=F32)


def dot(a, b):
    return jnp.dot(a, b, preferred_element_type=F32)


def causal_keep(n):
    return lax.broadcasted_iota(jnp.int32, (n, n), 0) <= lax.broadcasted_iota(jnp.int32, (n, n), 1)


def piece_range(c):
    return jnp.where(c == 2, 1, 0), jnp.where(c < 2, c, 3)


def fwd_kernel(cp_ref, qpre_ref, cos_ref, sin_ref, core_ref, x_ref, xc_ref, own_ref, q_ref, o_ref, lse_ref, m_scr, l_scr, acc_scr, k_scr, vt_scr):
    c = cp_ref[0]
    lo, hi = piece_range(c)
    keep = causal_keep(HALF)
    cos, sin = cos_ref[...], sin_ref[...]

    @pl.when(pl.program_id(1) == 0)
    def _():
        for n, ref in enumerate((core_ref, x_ref, xc_ref, own_ref)):
            def load(n=n, ref=ref):
                k_scr[n] = ref[0, :, :E]
                vt_scr[n] = ref[0, :, E:].T

            if n == 3:
                load()
            else:
                pl.when((n >= lo) & (n < hi))(load)

    qs = []
    for hh in range(HPF):
        cols = slice(hh * E, (hh + 1) * E)
        q = (rot(qpre_ref[0, :, cols], cos, sin) * (E ** -0.5)).astype(BF16)
        q_ref[0, :, cols] = q
        qs.append(q)

    def diag_scores(hh):
        q, k_d = qs[hh], k_scr[3]
        s_a = jnp.where(keep, dot_nt(k_d[:HALF], q[:HALF]), -jnp.inf)
        s_b = dot_nt(k_d[:HALF], q[HALF:])
        s_c = jnp.where(keep, dot_nt(k_d[HALF:], q[HALF:]), -jnp.inf)
        return s_a, s_b, s_c

    def diag_rest(hh, scores):
        s_a, s_b, s_c = scores
        m_a = jnp.max(s_a, axis=0, keepdims=True)
        m_b = jnp.maximum(jnp.max(s_b, axis=0, keepdims=True), jnp.max(s_c, axis=0, keepdims=True))
        p_a = jnp.exp(s_a - m_a)
        p_b = jnp.exp(s_b - m_b)
        p_c = jnp.exp(s_c - m_b)
        m_scr[hh, :, :HALF] = m_a
        m_scr[hh, :, HALF:] = m_b
        l_scr[hh, :, :HALF] = jnp.sum(p_a, axis=0, keepdims=True)
        l_scr[hh, :, HALF:] = jnp.sum(p_b, axis=0, keepdims=True) + jnp.sum(p_c, axis=0, keepdims=True)
        vt_d = vt_scr[3]
        acc_scr[hh, :, :HALF] = dot(vt_d[:, :HALF], p_a.astype(BF16))
        acc_scr[hh, :, HALF:] = dot(vt_d[:, :HALF], p_b.astype(BF16)) + dot(vt_d[:, HALF:], p_c.astype(BF16))

    nxt = diag_scores(0)
    for hh in range(HPF):
        cur = nxt
        if hh + 1 < HPF:
            nxt = diag_scores(hh + 1)
        diag_rest(hh, cur)

    def step(j, carry):
        def scores(hh):
            return dot_nt(k_scr[j], q_ref[0, :, hh * E:(hh + 1) * E])

        nxt = scores(0)
        for hh in range(HPF):
            s = nxt
            if hh + 1 < HPF:
                nxt = scores(hh + 1)
            m_old = m_scr[hh]
            m_new = jnp.maximum(m_old, jnp.max(s, axis=0, keepdims=True))
            alpha = jnp.exp(m_old - m_new)
            p = jnp.exp(s - m_new)
            m_scr[hh] = m_new
            l_scr[hh] = l_scr[hh] * alpha + jnp.sum(p, axis=0, keepdims=True)
            acc_scr[hh] = acc_scr[hh] * alpha + dot(vt_scr[j], p.astype(BF16))
        return carry

    lax.fori_loop(lo, hi, step, 0)
    for hh in range(HPF):
        l = l_scr[hh]
        o_ref[0, :, hh * E:(hh + 1) * E] = (acc_scr[hh] * (1.0 / l)).astype(BF16).T
        lse_ref[0, hh] = m_scr[hh] + jnp.log(l)


def attn_fwd(cp_arr, q_pre, cos, sin, pieces, b0, nb):
    width = q_pre.shape[2]
    n_hp = width // (HPF * E)
    wide = pl.BlockSpec((1, S, HPF * E), lambda b, h, cp: (b, 0, h))
    wide_in = pl.BlockSpec((1, S, HPF * E), lambda b, h, cp: (b + b0, 0, h))
    tab = pl.BlockSpec((S, E // 2), lambda b, h, cp: (0, 0))
    kv_spec = pl.BlockSpec((1, S, 2 * E), lambda b, h, cp: (b + b0, 0, 0))
    return pl.pallas_call(
        fwd_kernel,
        grid_spec=pltpu.PrefetchScalarGridSpec(
            num_scalar_prefetch=1,
            grid=(nb, n_hp),
            in_specs=[wide_in, tab, tab] + [kv_spec] * 4,
            out_specs=[wide, wide, pl.BlockSpec((1, HPF, 1, S), lambda b, h, cp: (b, h, 0, 0))],
            scratch_shapes=[pltpu.VMEM((HPF, 1, S), F32), pltpu.VMEM((HPF, 1, S), F32), pltpu.VMEM((HPF, E, S), F32),
                            pltpu.VMEM((4, S, E), BF16), pltpu.VMEM((4, E, S), BF16)]),
        out_shape=[jax.ShapeDtypeStruct((nb, S, width), BF16), jax.ShapeDtypeStruct((nb, S, width), BF16),
                   jax.ShapeDtypeStruct((nb, n_hp * HPF, 1, S), F32)],
        compiler_params=pltpu.CompilerParams(dimension_semantics=("arbitrary", "arbitrary"), vmem_limit_bytes=56 * 1024 * 1024),
        cost_estimate=pl.CostEstimate(flops=nb * 8 * 4 * 4 * S * S * E, bytes_accessed=nb * S * width * 8, transcendentals=0),
        name="attn_fwd",
    )(cp_arr, q_pre, cos, sin, *pieces)


def bwd_kernel(with_dkv, cp_ref, q_ref, do_ref, o_ref, lse_ref, cos_ref, sin_ref, core_ref, x_ref, xc_ref, own_ref, *rest):
    if with_dkv:
        dq_ref, dcore_ref, dx_ref, dxc_ref, down_ref, dl_scr, dqt_scr, k_scr, v_scr, kt_scr, dkv_scr = rest
        outs = (dcore_ref, dx_ref, dxc_ref, down_ref)
    else:
        dq_ref, dl_scr, dqt_scr, k_scr, v_scr, kt_scr = rest
        outs = (None,) * 4
    c = cp_ref[0]
    lo, hi = piece_range(c)
    keep = causal_keep(HALF)

    def each_piece(fn):
        for n, pair in enumerate(zip((core_ref, x_ref, xc_ref, own_ref), outs)):
            if n == 3:
                fn(n, *pair)
            else:
                pl.when((n >= lo) & (n < hi))(functools.partial(fn, n, *pair))

    @pl.when(pl.program_id(1) == 0)
    def _():
        def load(n, ref, out):
            k_scr[n] = ref[0, :, :E]
            v_scr[n] = ref[0, :, E:]
            kt_scr[n] = ref[0, :, :E].T
            if with_dkv:
                dkv_scr[n] = jnp.zeros((2, S, E), F32)

        each_piece(load)

    def cols(hh):
        return slice(hh * E, (hh + 1) * E)

    def scores(hh, j, ks, qs):
        s = dot_nt(k_scr[j, ks], q_ref[0, qs, cols(hh)])
        dp = dot_nt(v_scr[j, ks], do_ref[0, qs, cols(hh)])
        return s, dp

    def work(hh, sc, qs, masked):
        s, dp = sc
        p = jnp.exp(s - lse_ref[0, hh, :, qs])
        if masked:
            p = jnp.where(keep, p, 0.0)
        ds = (p * (dp - dl_scr[hh, :, qs])).astype(BF16)
        return p.astype(BF16), ds

    def grads(hh, j, p, ds, ks, qs):
        dqt_scr[hh, :, qs] += dot(kt_scr[j, :, ks], ds)
        if with_dkv:
            return dot(ds, q_ref[0, qs, cols(hh)]), dot(p, do_ref[0, qs, cols(hh)])
        return None

    def block(j, ks, qs, masked):
        nxt = scores(0, j, ks, qs)
        tot = None
        for hh in range(HPS):
            cur = nxt
            if hh + 1 < HPS:
                nxt = scores(hh + 1, j, ks, qs)
            p, ds = work(hh, cur, qs, masked)
            got = grads(hh, j, p, ds, ks, qs)
            if with_dkv:
                tot = got if tot is None else (tot[0] + got[0], tot[1] + got[1])
        if with_dkv:
            dkv_scr[j, 0, ks] += tot[0]
            dkv_scr[j, 1, ks] += tot[1]

    for hh in range(HPS):
        prod = do_ref[0, :, cols(hh)].astype(F32) * o_ref[0, :, cols(hh)].astype(F32)
        prod = prod[:, :E // 2] + prod[:, E // 2:]
        dl_scr[hh] = jnp.sum(prod.T, axis=0, keepdims=True)
        dqt_scr[hh] = jnp.zeros((E, S), F32)

    first, second = slice(0, HALF), slice(HALF, S)
    block(3, first, first, True)
    block(3, first, second, False)
    block(3, second, second, True)

    def step(j, carry):
        block(j, slice(0, S), slice(0, S), False)
        return carry

    lax.fori_loop(lo, hi, step, 0)
    for hh in range(HPS):
        dq = dqt_scr[hh].T
        dq_ref[0, :, cols(hh)] = (unrot(dq, cos_ref[...], sin_ref[...]) * (E ** -0.5)).astype(BF16)

    if with_dkv:
        @pl.when(pl.program_id(1) == pl.num_programs(1) - 1)
        def _():
            def store(n, ref, out):
                out[0, :, :E] = dkv_scr[n, 0]
                out[0, :, E:] = dkv_scr[n, 1]

            each_piece(store)


def attn_bwd(cp_arr, q, do, o, lse, cos, sin, pieces, b0, with_dkv=True):
    nb, _, width = q.shape
    n_hp = width // (HPS * E)
    wide = pl.BlockSpec((1, S, HPS * E), lambda b, h, cp: (b, 0, h))
    wide_in = pl.BlockSpec((1, S, HPS * E), lambda b, h, cp: (b + b0, 0, h))
    tab = pl.BlockSpec((S, E // 2), lambda b, h, cp: (0, 0))
    kv_spec = pl.BlockSpec((1, S, 2 * E), lambda b, h, cp: (b + b0, 0, 0))
    out_specs = [wide] + [pl.BlockSpec((1, S, 2 * E), lambda b, h, cp: (b, 0, 0))] * 4
    out_shape = [jax.ShapeDtypeStruct((nb, S, width), BF16)] + [jax.ShapeDtypeStruct((nb, S, 2 * E), F32)] * 4
    scratch = [pltpu.VMEM((HPS, 1, S), F32), pltpu.VMEM((HPS, E, S), F32), pltpu.VMEM((4, S, E), BF16),
               pltpu.VMEM((4, S, E), BF16), pltpu.VMEM((4, E, S), BF16), pltpu.VMEM((4, 2, S, E), F32)]
    n_out = 5 if with_dkv else 1
    res = pl.pallas_call(
        functools.partial(bwd_kernel, with_dkv),
        grid_spec=pltpu.PrefetchScalarGridSpec(
            num_scalar_prefetch=1,
            grid=(nb, n_hp),
            in_specs=[wide, wide_in, wide, pl.BlockSpec((1, HPS, 1, S), lambda b, h, cp: (b, h, 0, 0)), tab, tab] + [kv_spec] * 4,
            out_specs=out_specs[:n_out],
            scratch_shapes=scratch if with_dkv else scratch[:5]),
        out_shape=out_shape[:n_out],
        compiler_params=pltpu.CompilerParams(dimension_semantics=("arbitrary", "arbitrary"), vmem_limit_bytes=60 * 1024 * 1024),
        cost_estimate=pl.CostEstimate(flops=nb * 8 * 10 * 4 * S * S * E, bytes_accessed=nb * S * width * 8, transcendentals=0),
        name="attn_bwd" if with_dkv else "attn_bwd_dq",
    )(cp_arr, q, do, o, lse, cos, sin, *pieces)
    return res if with_dkv else res[0]


N_CHUNK = 4
SEQUENCE = (("f", 0), ("f", 1), ("b", 0), ("f", 2), ("b", 1), ("f", 3), ("b", 2), ("b", 3))
FINISH_AFTER = {0: 3, 1: 5, 2: 7}


def blank_kernel(o_ref):
    del o_ref


def blank(shape, dtype):
    return pl.pallas_call(blank_kernel, out_shape=jax.ShapeDtypeStruct(shape, dtype), out_specs=pl.BlockSpec(memory_space=pl.ANY))()


def solution(mesh):
    axes = ("tp", "cp")
    dev = lambda t, c: t * 4 + c
    Y = [(dev(t, c), dev(1 - t, c)) for t in range(2) for c in range(4)]
    CORE = [(dev(t, c), dev(t, c ^ 1)) for t in range(2) for c in range(4)]
    X = [(dev(t, c), dev(t, c ^ 2)) for t in range(2) for c in range(4)]
    XUP = [(dev(t, c), dev(t, c + 2)) for t in range(2) for c in range(2)]
    XDN = [(dev(t, c + 2), dev(t, c)) for t in range(2) for c in range(2)]
    ODD_DN = [(dev(t, c + 1), dev(t, c)) for t in range(2) for c in (0, 2)]
    CORE_HI = [(dev(t, c), dev(t, c ^ 1)) for t in range(2) for c in (2, 3)]

    def perm(x, pairs):
        return lax.ppermute(x, axes, pairs)

    def ein(spec, a, b, dtype=F32):
        return jnp.einsum(spec, a, b, preferred_element_type=F32).astype(dtype)

    def body(hidden, grad_out, w_query, w_key, w_value, w_out):
        t = lax.axis_index("tp")
        c = lax.axis_index("cp")
        core = c % 2
        xc = c // 2
        even = core == 0
        n_batch, _, d = hidden.shape
        nb = n_batch // 2
        cb = nb // N_CHUNK
        cp_arr = c.astype(jnp.int32).reshape(1)
        cos, sin = rope_tables(c * S + jnp.arange(S), E)
        wq_own = w_query.reshape(d, -1)
        wo_own = w_out.reshape(-1, d)
        n_own = wq_own.shape[1]
        w_kv = jnp.concatenate([w_key, w_value], axis=1)

        def fetch(w):
            rows = w.shape[0] // 2
            got = perm(lax.dynamic_slice_in_dim(w, core * rows, rows, 0), Y)
            other = perm(got, CORE)
            return jnp.where(even, jnp.concatenate([got, other], 0), jnp.concatenate([other, got], 0))

        wq_oth = fetch(wq_own)
        wo_oth = fetch(wo_own)
        w_q = jnp.concatenate([wq_own, wq_oth], axis=1)
        w_o = jnp.concatenate([wo_own, wo_oth], axis=0)

        h_own = lax.dynamic_slice_in_dim(hidden, t * nb, nb, 0)
        g_own = lax.dynamic_slice_in_dim(grad_out, t * nb, nb, 0)
        kv_pre = ein("bsd,de->bse", h_own, w_kv)
        kv_own = jnp.concatenate([rot(kv_pre[..., :E], cos, sin), kv_pre[..., E:]], axis=-1).astype(BF16)
        kv_core = perm(kv_own, CORE)
        kv_x = perm(kv_own, XUP)
        kv_xc = perm(kv_x, CORE_HI)
        pieces = (kv_core, kv_x, kv_xc, kv_own)

        def place(buf, val, col):
            return lax.dynamic_update_slice_in_dim(buf, val, col, 2)

        q_pre = place(blank((nb, S, 2 * n_own), F32), ein("bsd,de->bse", h_own, wq_own), 0)
        d_o = place(blank((nb, S, 2 * n_own), BF16), ein("bsd,ed->bse", g_own, wo_own, BF16), 0)
        q_pre = place(q_pre, ein("bsd,de->bse", h_own, wq_oth), n_own)
        d_o = place(d_o, ein("bsd,ed->bse", g_own, wo_oth, BF16), n_own)

        attn_out = blank(hidden.shape, BF16)
        d_hidden = blank(hidden.shape, BF16)
        gots, goths, fwd, bwd, dkv_parts = {}, {}, {}, {}, {}

        def finish(i, after):
            nonlocal d_hidden, q_pre, d_o
            tot = bwd[i][1]
            if after is not None:
                tot, after = lax.optimization_barrier((tot, after))
            dkv_pre = jnp.concatenate([unrot(tot[..., :E], cos, sin), tot[..., E:]], axis=-1).astype(BF16)
            d_h = (ein("bse,de->bsd", bwd[i][0], w_q) + ein("bse,de->bsd", dkv_pre, w_kv)).astype(BF16)
            q_pre, d_o, d_h = lax.optimization_barrier((q_pre, d_o, d_h))
            goths[i] = perm(d_h, Y)
            d_hidden = lax.dynamic_update_slice_in_dim(d_hidden, d_h, t * nb + i * cb, 0)
            dkv_parts[i] = dkv_pre
            return after

        for pos, (kind, i) in enumerate(SEQUENCE):
            if kind == "f":
                fwd[i] = attn_fwd(cp_arr, q_pre, cos, sin, pieces, i * cb, cb)
                out = ein("bse,ed->bsd", fwd[i][1], w_o, BF16)
                gots[i] = perm(out, Y)
                attn_out = lax.dynamic_update_slice_in_dim(attn_out, out, t * nb + i * cb, 0)
            else:
                q, o, lse = fwd[i]
                dq, d_core, d_x, d_xc, d_mine = attn_bwd(cp_arr, q, d_o, o, lse, cos, sin, pieces, i * cb)
                down = perm(d_core, ODD_DN)
                swap = perm(d_xc, CORE_HI)
                from_x = perm(d_x + swap, XDN)
                bwd[i] = (dq, d_mine + down + from_x)
            for k, at in FINISH_AFTER.items():
                if at == pos:
                    if kind == "f":
                        fwd[i] = (fwd[i][0], finish(k, fwd[i][1]), fwd[i][2])
                    else:
                        bwd[i] = (finish(k, bwd[i][0]), bwd[i][1])

        def pick(x, i, n):
            rows = x.shape[0] // n
            return lax.dynamic_slice_in_dim(x, i * rows, rows, 0)

        def join(first, a, b):
            return jnp.where(first, jnp.concatenate([a, b], 0), jnp.concatenate([b, a], 0))

        def reduce_w(own, oth):
            own = pick(own, core, 2) + perm(pick(own, 1 - core, 2), CORE)
            oth = pick(oth, core, 2) + perm(pick(oth, 1 - core, 2), CORE)
            oth = pick(oth, xc, 2) + perm(pick(oth, 1 - xc, 2), X)
            own = pick(own, xc, 2) + perm(pick(own, 1 - xc, 2), X)
            part = own + perm(oth, Y)
            half = join(xc == 0, part, perm(part, X))
            return join(even, half, perm(half, CORE))

        o_all = jnp.concatenate([fwd[i][1] for i in range(N_CHUNK)], 0)
        dq_all = jnp.concatenate([bwd[i][0] for i in range(N_CHUNK)], 0)
        two = [ein("bse,bsd->ed", o_all[..., k * n_own:(k + 1) * n_own], g_own) for k in range(2)]
        d_w_out = reduce_w(*two).reshape(w_out.shape)
        h_own, dq_all, _ = lax.optimization_barrier((h_own, dq_all, d_o))
        two = [ein("bsd,bse->de", h_own, dq_all[..., k * n_own:(k + 1) * n_own]) for k in range(2)]
        finish(N_CHUNK - 1, None)
        for i in range(N_CHUNK):
            attn_out = lax.dynamic_update_slice_in_dim(attn_out, gots[i], (1 - t) * nb + i * cb, 0)
            d_hidden = lax.dynamic_update_slice_in_dim(d_hidden, goths[i], (1 - t) * nb + i * cb, 0)
        dkv_all = jnp.concatenate([dkv_parts[i] for i in range(N_CHUNK)], 0)
        d_w_query = reduce_w(*two).reshape(w_query.shape)
        d_w_kv = lax.psum(ein("bsd,bse->de", h_own, dkv_all), axes)
        return attn_out, d_hidden, d_w_query, d_w_kv[:, :E], d_w_kv[:, E:], d_w_out

    row = P(None, "cp", None)
    return jax.shard_map(body, mesh=mesh, in_specs=(row, row, P(None, "tp", None), P(), P(), P("tp", None, None)), out_specs=(row, row, P(None, "tp", None), P(), P(), P("tp", None, None)), check_vma=False)
```

time: 5980 us -> 1750 us (0.29)
  waiting for transfers between devices: 3130 us -> 941 us
  blocking collectives: 1510 us -> 0 us
  matrix products: 642 us -> 349 us
  local copies, waits for them, and re-layouts: 308 us -> 148 us
  starting transfers between devices: 195 us -> 45.4 us
  Pallas kernels: 0 us -> 137 us
    psum x2 -> x1, waiting for transfers between devices: 1660 us -> 0.01 us  [body(): d_w_kv = lax.psum(ein('bsd,bse->de', h_own, dkv_all), axes)]
    psum x1 -> x0, blocking collectives: 1510 us -> none  [local_program(): attn_out = lax.psum(out_part, 'tp').astype(jnp.bfloat16)]
    ppermute x10 -> x41, waiting for transfers between devices: 1470 us -> 941 us  [perm(): return lax.ppermute(x, axes, pairs)]
    dot_general x19 -> x22, matrix products: 642 us -> 349 us  [ein(): return jnp.einsum(spec, a, b, preferred_element_type=F32).astype(dtype)]
    ppermute x10 -> x41, starting transfers between devices: 195 us -> 45.4 us  [perm(): return lax.ppermute(x, axes, pairs)]
    pallas_call x0 -> x12, Pallas kernels: none -> 137 us  [the longest x4 88 us: attn_bwd(): pl.pallas_call(functools.partial(bwd_kernel, with_dkv), grid_spec=pltpu.P...]
    while x6 -> x0, local copies, waits for them, and re-layouts: 92.9 us -> none  [the longest x2 35.4 us: local_program(): lax.fori_loop(0, cp_size - 1, fwd_body, (kv_loc, stats_init))]
    another operation x8 -> x0, local copies, waits for them, and re-layouts: 68.6 us -> none
  transfers between devices with their start and end apart: 12 -> 42, of which waited for: 10 -> 15; matrix products, arithmetic and copies ran while one was open for 8% -> 29% of each run, Pallas kernels for 0% -> 5%
where the time goes in v1:
time: 1750 us; the launch traced here: 1740 us
  waiting for transfers between devices  941 us (54%)
  matrix products  349 us (20%)
  local copies, waits for them, and re-layouts  148 us (8%)
  Pallas kernels  137 us (8%)
  other arithmetic  102 us (6%)
  starting transfers between devices  45.4 us (3%)
    ppermute x41, waiting for transfers between devices, perm(): return lax.ppermute(x, axes, pairs)  941 us
    dot_general x22, matrix products, ein(): return jnp.einsum(spec, a, b, preferred_element_type=F32).astype(dtype)  349 us
    pallas_call x4, Pallas kernels, attn_bwd(): pl.pallas_call(functools.partial(bwd_kernel, with_dkv), grid_spec=pltpu.P...  88 us
    pallas_call x4, Pallas kernels, attn_fwd(): pl.pallas_call(fwd_kernel, grid_spec=pltpu.PrefetchScalarGridSpec(num_sca...  48.9 us
    ppermute x41, starting transfers between devices, perm(): return lax.ppermute(x, axes, pairs)  45.4 us
    select_n x5, other arithmetic, join(): jnp.where(first, jnp.concatenate([a, b], 0), jnp.concatenate([b, a], 0))  40.8 us
  transfers between devices with their start and end apart: 42, of which 15 were waited for; matrix products, arithmetic and copies ran while one was open for 29% of the time, Pallas kernels for 5%

profile of v1, /device:TPU:0, one launch (start us, length us, event | category | flops | bytes accessed | tf_op | source)
XLA Modules:
  0.0 1737.6 jit_solution(10649640057470447717)
XLA Ops:
  10.6 8.4 constant_dynamic-slice_fusion.10
  19.0 12.1 fusion.96
  39.8 7.5 collective-permute-start.3
  47.4 5.3 copy.51
  59.6 7.7 reshape.104
  67.3 23.4 %convolution_dynamic-update-slice_fusion.1 = f32[8,512,2048]{2,1,0:T(8,128)} fusion(f32[8,512,2048]{2,1,0:T(8,128)} %shard_map.110, bf16[8,512,2048]{2,1,0:T(8,128)(2,1)} %copy-done, bf16[2048,1024,1]{1,0,2:T(8,128)(2,1)} %reshape.104), kind=kOutput, calls=%fused_computation.2 | convolution fusion | flops 17179869184 | bytes 37748736 | tf_op jit(solution)/shard_map/bsd,de->bse/dot_general | solution.py:311
  90.7 56.8 %collective-permute-done.5 = bf16[512,2048]{1,0:T(8,128)(2,1)} collective-permute-done((bf16[512,2048]{1,0:T(8,128)(2,1)}, bf16[512,2048]{1,0:T(8,128)(2,1)}, u32[]{:S(2)}, u32[]{:S(2)}) %collective-permute-start.5) | collective-permute-done | bytes 2097184 | tf_op jit(solution)/shard_map/ppermute | solution.py:308
  147.5 23.9 %convert_dynamic-update-slice_fusion.1 = bf16[8,512,2048]{2,1,0:T(8,128)(2,1)} fusion(bf16[8,512,2048]{2,1,0:T(8,128)(2,1)} %shard_map.111, bf16[1024,2048,1]{1,0,2:T(8,128)(2,1)} %bitcast.91, bf16[16,512,2048]{2,1,0:T(8,128)(2,1)} %param.7, s32[]{:T(128)S(6)} %select_n.135), kind=kOutput, calls=%fused_computation.26 | convolution fusion | flops 17184063488 | bytes 29360132 | tf_op jit(solution)/shard_map/bsd,ed->bse/dot_general | solution.py:311
  177.1 24.2 %convert_dynamic-update-slice_fusion.do_ref = bf16[8,512,2048]{2,1,0:T(8,128)(2,1)} fusion(bf16[8,512,2048]{2,1,0:T(8,128)(2,1)} %convert_dynamic-update-slice_fusion.1, bf16[16,512,2048]{2,1,0:T(8,128)(2,1)} %param.7, s32[]{:T(128)S(6)} %select_n.135, bf16[1024,2048]{1,0:T(8,128)(2,1)S(1)} %maximum_select_fusion.3), kind=kOutput, calls=%fused_computation.25 | convolution fusion | flops 17184063488 | bytes 29360132 | tf_op jit(solution)/shard_map/bsd,ed->bse/dot_general | solution.py:311
  204.8 23.7 %convolution_dynamic-update-slice_fusion.qpre_ref = f32[8,512,2048]{2,1,0:T(8,128)} fusion(f32[8,512,2048]{2,1,0:T(8,128)} %convolution_dynamic-update-slice_fusion.1, bf16[8,512,2048]{2,1,0:T(8,128)(2,1)} %copy-done, bf16[2048,1024]{1,0:T(8,128)(2,1)S(1)} %maximum_select_fusion.2), kind=kOutput, calls=%fused_computation.1 | convolution fusion | flops 17179869184 | bytes 37748736 | tf_op jit(solution)/shard_map/bsd,de->bse/dot_general | solution.py:311
  230.5 12.4 attn_fwd.4
  242.8 22.1 %attn_bwd.4 = (bf16[2,512,2048]{2,1,0:T(8,128)(2,1)}, f32[2,512,512]{2,1,0:T(8,128)}, f32[2,512,512]{2,1,0:T(8,128)}, f32[2,512,512]{2,1,0:T(8,128)}, f32[2,512,512]{2,1,0:T(8,128)}) custom-call(s32[1]{0:T(128)} %bitcast.cp_ref, bf16[2,512,2048]{2,1,0:T(8,128)(2,1)} %get-tuple-element.57.q_ref, ...), custom_call_target="tpu_custom_call" | custom-call | flops 42949672960 | bytes 16777216 | tf_op jit(solution)/shard_map/attn_bwd/pallas_call | solution.py:267
  272.0 12.2 attn_fwd.5
  284.2 12.2 attn_fwd.6
  296.3 88.3 %collective-permute-done.9 = f32[2,512,512]{2,1,0:T(8,128)S(1)} collective-permute-done((f32[2,512,512]{2,1,0:T(8,128)S(1)}, f32[2,512,512]{2,1,0:T(8,128)S(1)}, u32[]{:S(2)}, u32[]{:S(2)}) %collective-permute-start.9) | collective-permute-done | bytes 2097184 | tf_op jit(solution)/shard_map/ppermute | solution.py:308
  387.5 5.7 fusion.63
  393.2 13.6 add_convert_fusion.3
  406.8 21.9 %attn_bwd.5 = (bf16[2,512,2048]{2,1,0:T(8,128)(2,1)}, f32[2,512,512]{2,1,0:T(8,128)}, f32[2,512,512]{2,1,0:T(8,128)}, f32[2,512,512]{2,1,0:T(8,128)}, f32[2,512,512]{2,1,0:T(8,128)}) custom-call(s32[1]{0:T(128)} %bitcast.cp_ref, bf16[2,512,2048]{2,1,0:T(8,128)(2,1)} %get-tuple-element.69.q_ref, ...), custom_call_target="tpu_custom_call" | custom-call | flops 42949672960 | bytes 16777216 | tf_op jit(solution)/shard_map/attn_bwd/pallas_call | solution.py:267
  429.7 15.5 constant_dynamic-update-slice_fusion.19
  450.1 10.7 constant_dynamic-update-slice_fusion.18
  469.2 12.1 attn_fwd.7
  481.4 98.1 %collective-permute-done.16 = f32[2,512,512]{2,1,0:T(8,128)} collective-permute-done((f32[2,512,512]{2,1,0:T(8,128)S(1)}, f32[2,512,512]{2,1,0:T(8,128)}, u32[]{:S(2)}, u32[]{:S(2)}) %collective-permute-start.16) | collective-permute-done | bytes 2097184 | tf_op jit(solution)/shard_map/ppermute | solution.py:308
  582.9 5.7 fusion.69
  588.6 13.4 add_convert_fusion.2
  602.0 22.1 %attn_bwd.6 = (bf16[2,512,2048]{2,1,0:T(8,128)(2,1)}, f32[2,512,512]{2,1,0:T(8,128)}, f32[2,512,512]{2,1,0:T(8,128)}, f32[2,512,512]{2,1,0:T(8,128)}, f32[2,512,512]{2,1,0:T(8,128)}) custom-call(s32[1]{0:T(128)} %bitcast.cp_ref, bf16[2,512,2048]{2,1,0:T(8,128)(2,1)} %get-tuple-element.79.q_ref, ...), custom_call_target="tpu_custom_call" | custom-call | flops 42949672960 | bytes 16777216 | tf_op jit(solution)/shard_map/attn_bwd/pallas_call | solution.py:267
  626.3 4.8 constant_dynamic-update-slice_fusion
  631.1 21.9 %attn_bwd.7 = (bf16[2,512,2048]{2,1,0:T(8,128)(2,1)}, f32[2,512,512]{2,1,0:T(8,128)}, f32[2,512,512]{2,1,0:T(8,128)}, f32[2,512,512]{2,1,0:T(8,128)}, f32[2,512,512]{2,1,0:T(8,128)}) custom-call(s32[1]{0:T(128)} %bitcast.cp_ref, bf16[2,512,2048]{2,1,0:T(8,128)(2,1)} %get-tuple-element.87.q_ref, ...), custom_call_target="tpu_custom_call" | custom-call | flops 42949672960 | bytes 16777216 | tf_op jit(solution)/shard_map/attn_bwd/pallas_call | solution.py:267
  655.0 22.6 %fusion.24 = f32[1024,2048]{1,0:T(8,128)S(1)} fusion(bf16[16,512,2048]{2,1,0:T(8,128)(2,1)} %param.7, s32[]{:T(128)S(6)} %select_n.135, bf16[8,512,2048]{2,1,0:T(8,128)(2,1)} %constant_dynamic-update-slice_fusion), kind=kOutput, calls=%fused_computation.29 | convolution fusion | flops 17179869184 | bytes 33554436 | tf_op jit(solution)/shard_map/bse,bsd->ed/dot_general | solution.py:311
  686.2 22.6 %fusion.29 = f32[1024,2048]{1,0:T(8,128)S(1)} fusion(bf16[16,512,2048]{2,1,0:T(8,128)(2,1)} %param.7, s32[]{:T(128)S(6)} %select_n.135, bf16[8,512,2048]{2,1,0:T(8,128)(2,1)} %constant_dynamic-update-slice_fusion), kind=kOutput, calls=%fused_computation.30 | convolution fusion | flops 17179869184 | bytes 33554436 | tf_op jit(solution)/shard_map/bse,bsd->ed/dot_general | solution.py:311
  716.0 101.7 %collective-permute-done.19 = f32[2,512,512]{2,1,0:T(8,128)S(1)} collective-permute-done((f32[2,512,512]{2,1,0:T(8,128)S(1)}, f32[2,512,512]{2,1,0:T(8,128)S(1)}, u32[]{:S(2)}, u32[]{:S(2)}) %collective-permute-start.19) | collective-permute-done | bytes 2097184 | tf_op jit(solution)/shard_map/ppermute | solution.py:308
  821.6 41.0 %collective-permute-done.22 = f32[2,512,512]{2,1,0:T(8,128)S(1)} collective-permute-done((f32[2,512,512]{2,1,0:T(8,128)S(1)}, f32[2,512,512]{2,1,0:T(8,128)S(1)}, u32[]{:S(2)}, u32[]{:S(2)}) %collective-permute-start.22) | collective-permute-done | bytes 2097184 | tf_op jit(solution)/shard_map/ppermute | solution.py:308
  867.4 6.9 pad_maximum_fusion
  874.3 5.7 fusion.75
  880.1 15.8 add_convert_fusion.1
  895.9 24.3 %fusion.21 = f32[2048,1024]{0,1:T(8,128)} fusion(bf16[8,512,2048]{2,1,0:T(8,128)(2,1)} %copy-done, bf16[8,512,2048]{2,1,0:T(8,128)(2,1)} %pad_maximum_fusion), kind=kOutput, calls=%fused_computation.28 | convolution fusion | flops 17179869184 | bytes 33554432 | tf_op jit(solution)/shard_map/bsd,bse->de/dot_general | solution.py:311
  920.2 4.8 constant_dynamic-slice_fusion.5
  925.4 21.6 %fusion.18 = f32[2048,1024]{0,1:T(8,128)} fusion(bf16[8,512,2048]{2,1,0:T(8,128)(2,1)S(1)} %bitcast.77, bf16[8,512,2048]{2,1,0:T(8,128)(2,1)} %pad_maximum_fusion), kind=kOutput, calls=%fused_computation.27 | convolution fusion | flops 17179869184 | bytes 33554432 | tf_op jit(solution)/shard_map/bsd,bse->de/dot_general | solution.py:311
  947.1 4.9 constant_dynamic-slice_fusion.7
  964.9 14.2 constant_dynamic-update-slice_fusion.17
  983.6 23.2 %collective-permute-done.37 = f32[256,2048]{1,0:T(8,128)} collective-permute-done((f32[256,2048]{1,0:T(8,128)}, f32[256,2048]{1,0:T(8,128)}, u32[]{:S(2)}, u32[]{:S(2)}) %collective-permute-start.37) | collective-permute-done | bytes 2097184 | tf_op jit(solution)/shard_map/ppermute | solution.py:308
  1017.8 34.0 %collective-permute-done.30 = f32[512,1024]{0,1:T(8,128)} collective-permute-done((f32[512,1024]{0,1:T(8,128)}, f32[512,1024]{0,1:T(8,128)}, u32[]{:S(2)}, u32[]{:S(2)}) %collective-permute-start.30) | collective-permute-done | bytes 2097184 | tf_op jit(solution)/shard_map/ppermute | solution.py:308
  1056.8 12.7 constant_dynamic-update-slice_fusion.16
  1069.9 26.8 %collective-permute-done.35 = f32[256,2048]{1,0:T(8,128)} collective-permute-done((f32[256,2048]{1,0:T(8,128)}, f32[256,2048]{1,0:T(8,128)}, u32[]{:S(2)}, u32[]{:S(2)}) %collective-permute-start.35) | collective-permute-done | bytes 2097184 | tf_op jit(solution)/shard_map/ppermute | solution.py:308
  1098.3 4.8 constant_dynamic-update-slice_fusion.11
  1107.9 4.9 constant_dynamic-update-slice_fusion.14
  1114.1 5.7 fusion.81
  1123.2 17.9 %collective-permute-done.28 = f32[512,1024]{0,1:T(8,128)} collective-permute-done((f32[512,1024]{0,1:T(8,128)}, f32[512,1024]{0,1:T(8,128)}, u32[]{:S(2)}, u32[]{:S(2)}) %collective-permute-start.28) | collective-permute-done | bytes 2097184 | tf_op jit(solution)/shard_map/ppermute | solution.py:308
  1145.5 14.9 add_convert_fusion
  1160.5 29.2 %collective-permute-done.39 = f32[256,2048]{1,0:T(8,128)} collective-permute-done((f32[256,2048]{1,0:T(8,128)S(1)}, f32[256,2048]{1,0:T(8,128)}, u32[]{:S(2)}, u32[]{:S(2)}) %collective-permute-start.39) | collective-permute-done | bytes 2097184 | tf_op jit(solution)/shard_map/ppermute | solution.py:308
  1191.3 5.2 maximum_select_fusion.6
  1196.9 86.8 %collective-permute-done.23 = bf16[2,512,2048]{2,1,0:T(8,128)(2,1)} collective-permute-done((bf16[2,512,2048]{2,1,0:T(8,128)(2,1)}, bf16[2,512,2048]{2,1,0:T(8,128)(2,1)}, u32[]{:S(2)}, u32[]{:S(2)}) %collective-permute-start.23) | collective-permute-done | bytes 4194336 | tf_op jit(solution)/shard_map/ppermute | solution.py:308
  1286.7 17.1 fusion.60
  1303.8 5.3 maximum_select_fusion.5
  1309.1 108.7 %collective-permute-done.13 = bf16[2,512,2048]{2,1,0:T(8,128)(2,1)} collective-permute-done((bf16[2,512,2048]{2,1,0:T(8,128)(2,1)}, bf16[2,512,2048]{2,1,0:T(8,128)(2,1)}, u32[]{:S(2)}, u32[]{:S(2)}) %collective-permute-start.13) | collective-permute-done | bytes 4194336 | tf_op jit(solution)/shard_map/ppermute | solution.py:308
  1417.8 4.8 constant_dynamic-update-slice_fusion.13
  1444.0 64.4 %collective-permute-done.24 = bf16[2,512,2048]{2,1,0:T(8,128)(2,1)} collective-permute-done((bf16[2,512,2048]{2,1,0:T(8,128)(2,1)}, bf16[2,512,2048]{2,1,0:T(8,128)(2,1)}, u32[]{:S(2)}, u32[]{:S(2)}) %collective-permute-start.24) | collective-permute-done | bytes 4194336 | tf_op jit(solution)/shard_map/ppermute | solution.py:308
  1508.4 4.9 constant_dynamic-update-slice_fusion.6
  1517.9 80.4 %collective-permute-done.25 = bf16[2,512,2048]{2,1,0:T(8,128)(2,1)} collective-permute-done((bf16[2,512,2048]{2,1,0:T(8,128)(2,1)}, bf16[2,512,2048]{2,1,0:T(8,128)(2,1)}, u32[]{:S(2)}, u32[]{:S(2)}) %collective-permute-start.25) | collective-permute-done | bytes 4194336 | tf_op jit(solution)/shard_map/ppermute | solution.py:308
  1598.3 4.8 constant_dynamic-update-slice_fusion.5
  1603.1 83.5 %collective-permute-done.26 = bf16[2,512,2048]{2,1,0:T(8,128)(2,1)} collective-permute-done((bf16[2,512,2048]{2,1,0:T(8,128)(2,1)}, bf16[2,512,2048]{2,1,0:T(8,128)(2,1)}, u32[]{:S(2)}, u32[]{:S(2)}) %collective-permute-start.26) | collective-permute-done | bytes 4194336 | tf_op jit(solution)/shard_map/ppermute | solution.py:308
  1693.2 9.6 maximum_select_fusion.1
  1704.6 5.6 maximum_select_fusion.4
  1710.3 5.3 copy.29
  1715.5 15.1 maximum_select_fusion
  (284 shorter events, 174.6 us)
Async XLA Ops:
  7.2 1506.2 %all-reduce.2.cloned.1.call-start = ((), (), s32[]{:S(2)}) async-start(), calls=%async_computation | async-start | bytes 8388608 | tf_op jit(solution)/shard_map/psum | solution.py:422
  39.8 132.1 %collective-permute-start.3 = (bf16[8,512,512]{2,1,0:T(8,128)(2,1)}, bf16[8,512,512]{2,1,0:T(8,128)(2,1)}, u32[]{:S(2)}, u32[]{:S(2)}) collective-permute-start(bf16[8,512,512]{2,1,0:T(8,128)(2,1)} %pad_maximum_fusion.1.own_ref), channel_id=1, source_target_pairs={{0,2},{1,3},{4,6},{5,7}} | collective-permute-start | bytes 12582920 | tf_op jit(solution)/shard_map/ppermute | solution.py:308
  47.4 181.1 %collective-permute-start.2 = (bf16[8,512,512]{2,1,0:T(8,128)(2,1)}, bf16[8,512,512]{2,1,0:T(8,128)(2,1)}, u32[]{:S(2)}, u32[]{:S(2)}) collective-permute-start(bf16[8,512,512]{2,1,0:T(8,128)(2,1)} %pad_maximum_fusion.1.own_ref), channel_id=1, source_target_pairs={{0,1},{1,0},{2,3},{3,2},{4,5},{5,4},{6,7},{7,6}} | collective-permute-start | bytes 12582920 | tf_op jit(solution)/shard_map/ppermute | solution.py:308
  54.4 117.0 %collective-permute-start = (bf16[1024,1024]{1,0:T(8,128)(2,1)S(1)}, bf16[1024,1024]{1,0:T(8,128)(2,1)}, u32[]{:S(2)}, u32[]{:S(2)}) collective-permute-start(bf16[1024,1024]{1,0:T(8,128)(2,1)S(1)} %constant_dynamic-slice_fusion.9), channel_id=1, source_target_pairs={{0,4},{1,5},{2,6},{3,7},{4,0},{5,1},{6,2},{7,3}} | collective-permute-start | bytes 6291464 | tf_op jit(solution)/shard_map/ppermute | solution.py:308
  59.1 88.4 %collective-permute-start.5 = (bf16[512,2048]{1,0:T(8,128)(2,1)}, bf16[512,2048]{1,0:T(8,128)(2,1)}, u32[]{:S(2)}, u32[]{:S(2)}) collective-permute-start(bf16[512,2048]{1,0:T(8,128)(2,1)} %constant_dynamic-slice_fusion.8), channel_id=1, source_target_pairs={{0,4},{1,5},{2,6},{3,7},{4,0},{5,1},{6,2},{7,3}} | collective-permute-start | bytes 6291464 | tf_op jit(solution)/shard_map/ppermute | solution.py:308
  147.5 25.6 %collective-permute-start.6 = (bf16[512,2048]{1,0:T(8,128)(2,1)}, bf16[512,2048]{1,0:T(8,128)(2,1)S(1)}, u32[]{:S(2)}, u32[]{:S(2)}) collective-permute-start(bf16[512,2048]{1,0:T(8,128)(2,1)} %collective-permute-done.5), channel_id=1, source_target_pairs={{0,1},{1,0},{2,3},{3,2},{4,5},{5,4},{6,7},{7,6}} | collective-permute-start | bytes 6291464 | tf_op jit(solution)/shard_map/ppermute | solution.py:308
  171.5 29.9 %collective-permute-start.1 = (bf16[1024,1024]{1,0:T(8,128)(2,1)}, bf16[1024,1024]{1,0:T(8,128)(2,1)S(1)}, u32[]{:S(2)}, u32[]{:S(2)}) collective-permute-start(bf16[1024,1024]{1,0:T(8,128)(2,1)} %collective-permute-done), channel_id=1, source_target_pairs={{0,1},{1,0},{2,3},{3,2},{4,5},{5,4},{6,7},{7,6}} | collective-permute-start | bytes 6291464 | tf_op jit(solution)/shard_map/ppermute | solution.py:308
  172.0 56.5 %collective-permute-start.4 = (bf16[8,512,512]{2,1,0:T(8,128)(2,1)}, bf16[8,512,512]{2,1,0:T(8,128)(2,1)S(1)}, u32[]{:S(2)}, u32[]{:S(2)}) collective-permute-start(bf16[8,512,512]{2,1,0:T(8,128)(2,1)} %collective-permute-done.3.x_ref), channel_id=1, source_target_pairs={{2,3},{3,2},{6,7},{7,6}} | collective-permute-start | bytes 12582920 | tf_op jit(solution)/shard_map/ppermute | solution.py:308
  177.1 24.3 %copy-start.20 = (bf16[1024,2048]{1,0:T(8,128)(2,1)}, bf16[1024,2048]{1,0:T(8,128)(2,1)S(1)}, u32[]{:S(2)}) copy-start(bf16[1024,2048]{1,0:T(8,128)(2,1)S(1)} %maximum_select_fusion.3) | copy-start | bytes 12582916
  204.8 23.7 %copy-start.17 = (bf16[2048,1024]{1,0:T(8,128)(2,1)}, bf16[2048,1024]{1,0:T(8,128)(2,1)S(1)}, u32[]{:S(2)}) copy-start(bf16[2048,1024]{1,0:T(8,128)(2,1)S(1)} %maximum_select_fusion.2) | copy-start | bytes 12582916
  264.9 3.5 collective-permute-start.8
  267.0 29.3 %collective-permute-start.7 = (f32[2,512,512]{2,1,0:T(8,128)}, f32[2,512,512]{2,1,0:T(8,128)}, u32[]{:S(2)}, u32[]{:S(2)}) collective-permute-start(f32[2,512,512]{2,1,0:T(8,128)} %get-tuple-element.61), channel_id=1, source_target_pairs={{1,0},{3,2},{5,4},{7,6}} | collective-permute-start | bytes 6291464 | tf_op jit(solution)/shard_map/ppermute | solution.py:308
  270.7 114.0 %collective-permute-start.9 = (f32[2,512,512]{2,1,0:T(8,128)S(1)}, f32[2,512,512]{2,1,0:T(8,128)S(1)}, u32[]{:S(2)}, u32[]{:S(2)}) collective-permute-start(f32[2,512,512]{2,1,0:T(8,128)S(1)} %add.226), channel_id=1, source_target_pairs={{2,0},{3,1},{6,4},{7,5}} | collective-permute-start | bytes 6291464 | tf_op jit(solution)/shard_map/ppermute | solution.py:308
  284.2 100.5 %copy-start.37 = (f32[2,512,512]{2,1,0:T(8,128)S(1)}, f32[2,512,512]{2,1,0:T(8,128)}, u32[]{:S(2)}) copy-start(f32[2,512,512]{2,1,0:T(8,128)} %get-tuple-element.60) | copy-start | bytes 6291460
  428.8 33.7 %collective-permute-start.15 = (f32[2,512,512]{2,1,0:T(8,128)}, f32[2,512,512]{2,1,0:T(8,128)S(1)}, u32[]{:S(2)}, u32[]{:S(2)}) collective-permute-start(f32[2,512,512]{2,1,0:T(8,128)} %get-tuple-element.75), channel_id=1, source_target_pairs={{2,3},{3,2},{6,7},{7,6}} | collective-permute-start | bytes 6291464 | tf_op jit(solution)/shard_map/ppermute | solution.py:308
  445.2 609.9 %collective-permute-start.10 = (bf16[2,512,2048]{2,1,0:T(8,128)(2,1)}, bf16[2,512,2048]{2,1,0:T(8,128)(2,1)}, u32[]{:S(2)}, u32[]{:S(2)}) collective-permute-start(bf16[2,512,2048]{2,1,0:T(8,128)(2,1)} %get-tuple-element.119), channel_id=1, source_target_pairs={{0,4},{1,5},{2,6},{3,7},{4,0},{5,1},{6,2},{7,3}} | collective-permute-start | bytes 12582920 | tf_op jit(solution)/shard_map/ppermute | solution.py:308
  460.8 20.6 %collective-permute-start.14 = (f32[2,512,512]{2,1,0:T(8,128)}, f32[2,512,512]{2,1,0:T(8,128)S(1)}, u32[]{:S(2)}, u32[]{:S(2)}) collective-permute-start(f32[2,512,512]{2,1,0:T(8,128)} %get-tuple-element.73), channel_id=1, source_target_pairs={{1,0},{3,2},{5,4},{7,6}} | collective-permute-start | bytes 6291464 | tf_op jit(solution)/shard_map/ppermute | solution.py:308
  463.0 116.5 %collective-permute-start.16 = (f32[2,512,512]{2,1,0:T(8,128)S(1)}, f32[2,512,512]{2,1,0:T(8,128)}, u32[]{:S(2)}, u32[]{:S(2)}) collective-permute-start(f32[2,512,512]{2,1,0:T(8,128)S(1)} %add.240), channel_id=1, source_target_pairs={{2,0},{3,1},{6,4},{7,5}} | collective-permute-start | bytes 6291464 | tf_op jit(solution)/shard_map/ppermute | solution.py:308
  469.2 110.2 %copy-start.40 = (f32[2,512,512]{2,1,0:T(8,128)S(1)}, f32[2,512,512]{2,1,0:T(8,128)}, u32[]{:S(2)}) copy-start(f32[2,512,512]{2,1,0:T(8,128)} %get-tuple-element.72) | copy-start | bytes 6291460
  481.4 98.1 %copy-start.41 = (f32[2,512,512]{2,1,0:T(8,128)}, f32[2,512,512]{2,1,0:T(8,128)S(1)}, u32[]{:S(2)}) copy-start(f32[2,512,512]{2,1,0:T(8,128)S(1)} %collective-permute-done.14) | copy-start | bytes 6291460
  624.2 58.3 %collective-permute-start.18 = (f32[2,512,512]{2,1,0:T(8,128)}, f32[2,512,512]{2,1,0:T(8,128)S(1)}, u32[]{:S(2)}, u32[]{:S(2)}) collective-permute-start(f32[2,512,512]{2,1,0:T(8,128)} %get-tuple-element.86), channel_id=1, source_target_pairs={{2,3},{3,2},{6,7},{7,6}} | collective-permute-start | bytes 6291464 | tf_op jit(solution)/shard_map/ppermute | solution.py:308
  625.0 89.4 %collective-permute-start.17 = (f32[2,512,512]{2,1,0:T(8,128)}, f32[2,512,512]{2,1,0:T(8,128)}, u32[]{:S(2)}, u32[]{:S(2)}) collective-permute-start(f32[2,512,512]{2,1,0:T(8,128)} %get-tuple-element.84), channel_id=1, source_target_pairs={{1,0},{3,2},{5,4},{7,6}} | collective-permute-start | bytes 6291464 | tf_op jit(solution)/shard_map/ppermute | solution.py:308
  652.9 31.4 %collective-permute-start.21 = (f32[2,512,512]{2,1,0:T(8,128)}, f32[2,512,512]{2,1,0:T(8,128)S(1)}, u32[]{:S(2)}, u32[]{:S(2)}) collective-permute-start(f32[2,512,512]{2,1,0:T(8,128)} %get-tuple-element.98), channel_id=1, source_target_pairs={{2,3},{3,2},{6,7},{7,6}} | collective-permute-start | bytes 6291464 | tf_op jit(solution)/shard_map/ppermute | solution.py:308
  653.7 167.8 %collective-permute-start.20 = (f32[2,512,512]{2,1,0:T(8,128)}, f32[2,512,512]{2,1,0:T(8,128)S(1)}, u32[]{:S(2)}, u32[]{:S(2)}) collective-permute-start(f32[2,512,512]{2,1,0:T(8,128)} %get-tuple-element.96), channel_id=1, source_target_pairs={{1,0},{3,2},{5,4},{7,6}} | collective-permute-start | bytes 6291464 | tf_op jit(solution)/shard_map/ppermute | solution.py:308
  682.9 134.8 %collective-permute-start.19 = (f32[2,512,512]{2,1,0:T(8,128)S(1)}, f32[2,512,512]{2,1,0:T(8,128)S(1)}, u32[]{:S(2)}, u32[]{:S(2)}) collective-permute-start(f32[2,512,512]{2,1,0:T(8,128)S(1)} %add.245), channel_id=1, source_target_pairs={{2,0},{3,1},{6,4},{7,5}} | collective-permute-start | bytes 6291464 | tf_op jit(solution)/shard_map/ppermute | solution.py:308
  684.9 177.8 %collective-permute-start.22 = (f32[2,512,512]{2,1,0:T(8,128)S(1)}, f32[2,512,512]{2,1,0:T(8,128)S(1)}, u32[]{:S(2)}, u32[]{:S(2)}) collective-permute-start(f32[2,512,512]{2,1,0:T(8,128)S(1)} %add.250), channel_id=1, source_target_pairs={{2,0},{3,1},{6,4},{7,5}} | collective-permute-start | bytes 6291464 | tf_op jit(solution)/shard_map/ppermute | solution.py:308
  708.8 110.2 %copy-start.38 = (f32[2,512,512]{2,1,0:T(8,128)S(1)}, f32[2,512,512]{2,1,0:T(8,128)}, u32[]{:S(2)}) copy-start(f32[2,512,512]{2,1,0:T(8,128)} %get-tuple-element.83) | copy-start | bytes 6291460
  708.8 153.9 %copy-start.39 = (f32[2,512,512]{2,1,0:T(8,128)S(1)}, f32[2,512,512]{2,1,0:T(8,128)}, u32[]{:S(2)}) copy-start(f32[2,512,512]{2,1,0:T(8,128)} %get-tuple-element.95) | copy-start | bytes 6291460
  714.3 355.1 %collective-permute-start.11 = (bf16[2,512,2048]{2,1,0:T(8,128)(2,1)}, bf16[2,512,2048]{2,1,0:T(8,128)(2,1)}, u32[]{:S(2)}, u32[]{:S(2)}) collective-permute-start(bf16[2,512,2048]{2,1,0:T(8,128)(2,1)} %get-tuple-element.121), channel_id=1, source_target_pairs={{0,4},{1,5},{2,6},{3,7},{4,0},{5,1},{6,2},{7,3}} | collective-permute-start | bytes 12582920 | tf_op jit(solution)/shard_map/ppermute | solution.py:308
  817.7 145.2 %collective-permute-start.34 = (f32[512,2048]{1,0:T(8,128)}, f32[512,2048]{1,0:T(8,128)}, u32[]{:S(2)}, u32[]{:S(2)}) collective-permute-start(f32[512,2048]{1,0:T(8,128)} %constant_dynamic-slice_fusion.3), channel_id=1, source_target_pairs={{0,1},{1,0},{2,3},{3,2},{4,5},{5,4},{6,7},{7,6}} | collective-permute-start | bytes 12582920 | tf_op jit(solution)/shard_map/ppermute | solution.py:308
  819.0 46.2 %copy-start.31 = (bf16[2,512,2048]{2,1,0:T(8,128)(2,1)S(1)}, bf16[2,512,2048]{2,1,0:T(8,128)(2,1)}, u32[]{:S(2)}) copy-start(bf16[2,512,2048]{2,1,0:T(8,128)(2,1)} %get-tuple-element.71) | copy-start | bytes 12582916
  819.0 46.2 %copy-start.32 = (bf16[2,512,2048]{2,1,0:T(8,128)(2,1)S(1)}, bf16[2,512,2048]{2,1,0:T(8,128)(2,1)}, u32[]{:S(2)}) copy-start(bf16[2,512,2048]{2,1,0:T(8,128)(2,1)} %get-tuple-element.82) | copy-start | bytes 12582916
  821.6 52.8 %copy-start.55 = (bf16[2,512,256]{2,1,0:T(8,128)(2,1)}, bf16[2,512,256]{2,1,0:T(8,128)(2,1)S(1)}, u32[]{:S(2)}) copy-start(bf16[2,512,256]{2,1,0:T(8,128)(2,1)S(1)} %slice.160) | copy-start | bytes 1572868
  821.6 130.4 %collective-permute-start.36 = (f32[512,2048]{1,0:T(8,128)}, f32[512,2048]{1,0:T(8,128)}, u32[]{:S(2)}, u32[]{:S(2)}) collective-permute-start(f32[512,2048]{1,0:T(8,128)} %constant_dynamic-slice_fusion.1), channel_id=1, source_target_pairs={{0,1},{1,0},{2,3},{3,2},{4,5},{5,4},{6,7},{7,6}} | collective-permute-start | bytes 12582920 | tf_op jit(solution)/shard_map/ppermute | solution.py:308
  880.1 45.3 %slice-start = ((s8[16777216]{0:T(1024)(128)(4,1)}), s8[4194304]{0:T(1024)(128)(4,1)S(1)}, s32[]{:S(2)}) async-start(s8[16777216]{0:T(1024)(128)(4,1)} %bitcast.76), calls=%async_computation.1 | async-start | bytes 8388608
  880.1 45.3 %slice-start.1 = ((s8[16777216]{0:T(1024)(128)(4,1)}), s8[4194304]{0:T(1024)(128)(4,1)S(1)}, s32[]{:S(2)}) async-start(s8[16777216]{0:T(1024)(128)(4,1)} %bitcast.76), calls=%async_computation.2 | async-start | bytes 8388608
  895.9 29.5 %slice-start.2 = ((s8[16777216]{0:T(1024)(128)(4,1)}), s8[4194304]{0:T(1024)(128)(4,1)S(1)}, s32[]{:S(2)}) async-start(s8[16777216]{0:T(1024)(128)(4,1)} %bitcast.76), calls=%async_computation.3 | async-start | bytes 8388608
  895.9 29.5 %slice-start.3 = ((s8[16777216]{0:T(1024)(128)(4,1)}), s8[4194304]{0:T(1024)(128)(4,1)S(1)}, s32[]{:S(2)}) async-start(s8[16777216]{0:T(1024)(128)(4,1)} %bitcast.76), calls=%async_computation.4 | async-start | bytes 8388608
  925.0 33.0 %collective-permute-start.29 = (f32[1024,1024]{0,1:T(8,128)}, f32[1024,1024]{0,1:T(8,128)}, u32[]{:S(2)}, u32[]{:S(2)}) collective-permute-start(f32[1024,1024]{0,1:T(8,128)} %constant_dynamic-slice_fusion.5), channel_id=1, source_target_pairs={{0,1},{1,0},{2,3},{3,2},{4,5},{5,4},{6,7},{7,6}} | collective-permute-start | bytes 12582920 | tf_op jit(solution)/shard_map/ppermute | solution.py:308
  952.0 58.1 %collective-permute-start.27 = (f32[1024,1024]{0,1:T(8,128)}, f32[1024,1024]{0,1:T(8,128)}, u32[]{:S(2)}, u32[]{:S(2)}) collective-permute-start(f32[1024,1024]{0,1:T(8,128)} %constant_dynamic-slice_fusion.7), channel_id=1, source_target_pairs={{0,1},{1,0},{2,3},{3,2},{4,5},{5,4},{6,7},{7,6}} | collective-permute-start | bytes 12582920 | tf_op jit(solution)/shard_map/ppermute | solution.py:308
  958.0 48.8 %collective-permute-start.37 = (f32[256,2048]{1,0:T(8,128)}, f32[256,2048]{1,0:T(8,128)}, u32[]{:S(2)}, u32[]{:S(2)}) collective-permute-start(f32[256,2048]{1,0:T(8,128)} %constant_dynamic-slice_fusion), channel_id=1, source_target_pairs={{0,2},{1,3},{2,0},{3,1},{4,6},{5,7},{6,4},{7,5}} | collective-permute-start | bytes 6291464 | tf_op jit(solution)/shard_map/ppermute | solution.py:308
  962.9 88.9 %collective-permute-start.30 = (f32[512,1024]{0,1:T(8,128)}, f32[512,1024]{0,1:T(8,128)}, u32[]{:S(2)}, u32[]{:S(2)}) collective-permute-start(f32[512,1024]{0,1:T(8,128)} %constant_dynamic-slice_fusion.4), channel_id=1, source_target_pairs={{0,2},{1,3},{2,0},{3,1},{4,6},{5,7},{6,4},{7,5}} | collective-permute-start | bytes 6291464 | tf_op jit(solution)/shard_map/ppermute | solution.py:308
  1006.8 89.9 %collective-permute-start.35 = (f32[256,2048]{1,0:T(8,128)}, f32[256,2048]{1,0:T(8,128)}, u32[]{:S(2)}, u32[]{:S(2)}) collective-permute-start(f32[256,2048]{1,0:T(8,128)} %constant_dynamic-slice_fusion.2), channel_id=1, source_target_pairs={{0,2},{1,3},{2,0},{3,1},{4,6},{5,7},{6,4},{7,5}} | collective-permute-start | bytes 6291464 | tf_op jit(solution)/shard_map/ppermute | solution.py:308
  1010.1 109.8 %collective-permute-start.38 = (f32[256,2048]{1,0:T(8,128)}, f32[256,2048]{1,0:T(8,128)}, u32[]{:S(2)}, u32[]{:S(2)}) collective-permute-start(f32[256,2048]{1,0:T(8,128)} %dynamic-slice_add_fusion.4), channel_id=1, source_target_pairs={{0,4},{1,5},{2,6},{3,7},{4,0},{5,1},{6,2},{7,3}} | collective-permute-start | bytes 6291464 | tf_op jit(solution)/shard_map/ppermute | solution.py:308
  1016.1 40.6 %copy-start.26 = (bf16[2,512,2048]{2,1,0:T(8,128)(2,1)S(1)}, bf16[2,512,2048]{2,1,0:T(8,128)(2,1)}, u32[]{:S(2)}) copy-start(bf16[2,512,2048]{2,1,0:T(8,128)(2,1)} %get-tuple-element.88.o_ref) | copy-start | bytes 12582916
  1017.8 39.0 %copy-start.23 = (bf16[1024,2048]{1,0:T(8,128)(2,1)S(1)}, bf16[1024,2048]{1,0:T(8,128)(2,1)}, u32[]{:S(2)}) copy-start(bf16[1024,2048]{1,0:T(8,128)(2,1)} %copy-done.20) | copy-start | bytes 12582916
  1051.7 89.4 %collective-permute-start.28 = (f32[512,1024]{0,1:T(8,128)}, f32[512,1024]{0,1:T(8,128)}, u32[]{:S(2)}, u32[]{:S(2)}) collective-permute-start(f32[512,1024]{0,1:T(8,128)} %constant_dynamic-slice_fusion.6), channel_id=1, source_target_pairs={{0,2},{1,3},{2,0},{3,1},{4,6},{5,7},{6,4},{7,5}} | collective-permute-start | bytes 6291464 | tf_op jit(solution)/shard_map/ppermute | solution.py:308
  1055.1 86.2 %collective-permute-start.31 = (f32[512,1024]{0,1:T(8,128)}, f32[512,1024]{0,1:T(8,128)S(1)}, u32[]{:S(2)}, u32[]{:S(2)}) collective-permute-start(f32[512,1024]{0,1:T(8,128)} %dynamic-slice_add_fusion.5), channel_id=1, source_target_pairs={{0,4},{1,5},{2,6},{3,7},{4,0},{5,1},{6,2},{7,3}} | collective-permute-start | bytes 6291464 | tf_op jit(solution)/shard_map/ppermute | solution.py:308
  1069.4 127.1 %collective-permute-start.12 = (bf16[2,512,2048]{2,1,0:T(8,128)(2,1)}, bf16[2,512,2048]{2,1,0:T(8,128)(2,1)}, u32[]{:S(2)}, u32[]{:S(2)}) collective-permute-start(bf16[2,512,2048]{2,1,0:T(8,128)(2,1)} %get-tuple-element.123), channel_id=1, source_target_pairs={{0,4},{1,5},{2,6},{3,7},{4,0},{5,1},{6,2},{7,3}} | collective-permute-start | bytes 12582920 | tf_op jit(solution)/shard_map/ppermute | solution.py:308
  1096.7 187.0 %collective-permute-start.23 = (bf16[2,512,2048]{2,1,0:T(8,128)(2,1)}, bf16[2,512,2048]{2,1,0:T(8,128)(2,1)}, u32[]{:S(2)}, u32[]{:S(2)}) collective-permute-start(bf16[2,512,2048]{2,1,0:T(8,128)(2,1)} %add_convert_fusion.3), channel_id=1, source_target_pairs={{0,4},{1,5},{2,6},{3,7},{4,0},{5,1},{6,2},{7,3}} | collective-permute-start | bytes 12582920 | tf_op jit(solution)/shard_map/ppermute | solution.py:308
  1119.9 297.9 %collective-permute-start.13 = (bf16[2,512,2048]{2,1,0:T(8,128)(2,1)}, bf16[2,512,2048]{2,1,0:T(8,128)(2,1)}, u32[]{:S(2)}, u32[]{:S(2)}) collective-permute-start(bf16[2,512,2048]{2,1,0:T(8,128)(2,1)} %get-tuple-element.125), channel_id=1, source_target_pairs={{0,4},{1,5},{2,6},{3,7},{4,0},{5,1},{6,2},{7,3}} | collective-permute-start | bytes 12582920 | tf_op jit(solution)/shard_map/ppermute | solution.py:308
  1141.1 48.6 %collective-permute-start.39 = (f32[256,2048]{1,0:T(8,128)S(1)}, f32[256,2048]{1,0:T(8,128)}, u32[]{:S(2)}, u32[]{:S(2)}) collective-permute-start(f32[256,2048]{1,0:T(8,128)S(1)} %add_add_fusion), channel_id=1, source_target_pairs={{0,2},{1,3},{2,0},{3,1},{4,6},{5,7},{6,4},{7,5}} | collective-permute-start | bytes 6291464 | tf_op jit(solution)/shard_map/ppermute | solution.py:308
  1143.7 141.6 %collective-permute-start.32 = (f32[512,1024]{0,1:T(8,128)S(1)}, f32[512,1024]{0,1:T(8,128)S(1)}, u32[]{:S(2)}, u32[]{:S(2)}) collective-permute-start(f32[512,1024]{0,1:T(8,128)S(1)} %add_add_fusion.1), channel_id=1, source_target_pairs={{0,2},{1,3},{2,0},{3,1},{4,6},{5,7},{6,4},{7,5}} | collective-permute-start | bytes 6291464 | tf_op jit(solution)/shard_map/ppermute | solution.py:308
  1160.4 126.2 %copy-start.52 = (bf16[2,512,256]{2,1,0:T(8,128)(2,1)S(1)}, bf16[2,512,256]{2,1,0:T(8,128)(2,1)}, u32[]{:S(2)}) copy-start(bf16[2,512,256]{2,1,0:T(8,128)(2,1)} %copy-done.51) | copy-start | bytes 1572868
  1160.4 126.2 %copy-start.54 = (bf16[2,512,256]{2,1,0:T(8,128)(2,1)S(1)}, bf16[2,512,256]{2,1,0:T(8,128)(2,1)}, u32[]{:S(2)}) copy-start(bf16[2,512,256]{2,1,0:T(8,128)(2,1)} %copy-done.53) | copy-start | bytes 1572868
  1160.4 126.2 %copy-start.56 = (bf16[2,512,256]{2,1,0:T(8,128)(2,1)S(1)}, bf16[2,512,256]{2,1,0:T(8,128)(2,1)}, u32[]{:S(2)}) copy-start(bf16[2,512,256]{2,1,0:T(8,128)(2,1)} %copy-done.55) | copy-start | bytes 1572868
  1160.5 126.2 %copy-start.58 = (bf16[2,512,256]{2,1,0:T(8,128)(2,1)S(1)}, bf16[2,512,256]{2,1,0:T(8,128)(2,1)}, u32[]{:S(2)}) copy-start(bf16[2,512,256]{2,1,0:T(8,128)(2,1)} %copy-done.57) | copy-start | bytes 1572868
  1160.5 126.2 %copy-start.60 = (bf16[2,512,128]{2,1,0:T(8,128)(2,1)S(1)}, bf16[2,512,128]{2,1,0:T(8,128)(2,1)}, u32[]{:S(2)}) copy-start(bf16[2,512,128]{2,1,0:T(8,128)(2,1)} %get-tuple-element.106) | copy-start | bytes 786436
  1189.7 318.7 %collective-permute-start.24 = (bf16[2,512,2048]{2,1,0:T(8,128)(2,1)}, bf16[2,512,2048]{2,1,0:T(8,128)(2,1)}, u32[]{:S(2)}, u32[]{:S(2)}) collective-permute-start(bf16[2,512,2048]{2,1,0:T(8,128)(2,1)} %add_convert_fusion.2), channel_id=1, source_target_pairs={{0,4},{1,5},{2,6},{3,7},{4,0},{5,1},{6,2},{7,3}} | collective-permute-start | bytes 12582920 | tf_op jit(solution)/shard_map/ppermute | solution.py:308
  1196.5 401.8 %collective-permute-start.25 = (bf16[2,512,2048]{2,1,0:T(8,128)(2,1)}, bf16[2,512,2048]{2,1,0:T(8,128)(2,1)}, u32[]{:S(2)}, u32[]{:S(2)}) collective-permute-start(bf16[2,512,2048]{2,1,0:T(8,128)(2,1)} %add_convert_fusion.1), channel_id=1, source_target_pairs={{0,4},{1,5},{2,6},{3,7},{4,0},{5,1},{6,2},{7,3}} | collective-permute-start | bytes 12582920 | tf_op jit(solution)/shard_map/ppermute | solution.py:308
  1283.7 402.8 %collective-permute-start.26 = (bf16[2,512,2048]{2,1,0:T(8,128)(2,1)}, bf16[2,512,2048]{2,1,0:T(8,128)(2,1)}, u32[]{:S(2)}, u32[]{:S(2)}) collective-permute-start(bf16[2,512,2048]{2,1,0:T(8,128)(2,1)} %add_convert_fusion), channel_id=1, source_target_pairs={{0,4},{1,5},{2,6},{3,7},{4,0},{5,1},{6,2},{7,3}} | collective-permute-start | bytes 12582920 | tf_op jit(solution)/shard_map/ppermute | solution.py:308
  1286.6 406.6 %collective-permute-start.40 = (f32[512,2048]{1,0:T(8,128)}, f32[512,2048]{1,0:T(8,128)}, u32[]{:S(2)}, u32[]{:S(2)}) collective-permute-start(f32[512,2048]{1,0:T(8,128)} %maximum_select_fusion.6), channel_id=1, source_target_pairs={{0,1},{1,0},{2,3},{3,2},{4,5},{5,4},{6,7},{7,6}} | collective-permute-start | bytes 12582920 | tf_op jit(solution)/shard_map/ppermute | solution.py:308
  1309.1 113.5 %copy-start.24 = (bf16[2,512,2048]{2,1,0:T(8,128)(2,1)S(1)}, bf16[2,512,2048]{2,1,0:T(8,128)(2,1)}, u32[]{:S(2)}) copy-start(bf16[2,512,2048]{2,1,0:T(8,128)(2,1)} %add_convert_fusion.2) | copy-start | bytes 12582916
  1417.8 292.5 %collective-permute-start.33 = (f32[1024,1024]{0,1:T(8,128)}, f32[1024,1024]{0,1:T(8,128)}, u32[]{:S(2)}, u32[]{:S(2)}) collective-permute-start(f32[1024,1024]{0,1:T(8,128)} %maximum_select_fusion.5), channel_id=1, source_target_pairs={{0,1},{1,0},{2,3},{3,2},{4,5},{5,4},{6,7},{7,6}} | collective-permute-start | bytes 12582920 | tf_op jit(solution)/shard_map/ppermute | solution.py:308
  (55 other events, 360.2 us)
Sparse Core Ops, SparseCore 0:
  1304.0 115.7 all-reduce.1
